TPU v7x, 32 devices: a whole 2x2x4 slice. The times are simulated.
32 devices in a mesh: gx: 4 (over y, x), gy: 2 (over core), gz: 4 (over z).
Axes of the slice: x: 2, y: 2, z: 4, core: 2. Of those that a mesh axis runs over, the one named last changes fastest.
Arguments:
- rhs: float32 [8, 64, 64, 512], P(None, 'gx', 'gy', 'gz'), may hold values from -8 to 8
- stencil: float32 [14, 64, 64, 512], P(None, 'gx', 'gy', 'gz'), may hold values from 0.02 to 1
Outputs:
- solution: float32 [8, 64, 64, 512], P(None, 'gx', 'gy', 'gz')
- residual: float32 [8, 64, 64, 512], P(None, 'gx', 'gy', 'gz')
All inputs are finite; a program needn't handle non-finite values.
Results may differ from a plain program's by a relative error of at most 0.00029.
Values sent between devices are 32-bit elements; how exact they have to be, the bound alone decides.
A program may use at most 128 MiB of HBM per device.

v0:
```python
import jax
import jax.numpy as jnp
from jax import lax
from jax.experimental import pallas as pl
from jax.experimental.pallas import tpu as pltpu
from jax.sharding import PartitionSpec as P

FORWARD = [
    (a, b, c) for a in (-1, 0, 1) for b in (-1, 0, 1) for c in (-1, 0, 1) if (a, b, c) > (0, 0, 0)
]
AXES = ("gx", "gy", "gz")
LO = [k for k, o in enumerate(FORWARD) if o[2] == 1]
HI = [k for k, o in enumerate(FORWARD) if o[2] == -1]
EX = [k for k, o in enumerate(FORWARD) if o[0] == 1]
F32 = jnp.float32


def runs(ks):
    out = []
    for k in ks:
        if out and out[-1][1] == k:
            out[-1][1] = k + 1
        else:
            out.append([k, k + 1])
    return out


def mm(a, b):
    total = a[:, 0:1] * b[0:1, :]
    for k in range(1, 8):
        total = total + a[:, k : k + 1] * b[k : k + 1, :]
    return total


def solve(matrix, right, row):
    aug = matrix + pltpu.roll(right, 8, 1)
    for k in range(8):
        pivot = aug[k : k + 1, :] / aug[k : k + 1, k : k + 1]
        aug = jnp.where(row == k, pivot, aug - aug[:, k : k + 1] * pivot)
    return pltpu.roll(aug, 120, 1)


def transposed(a, row, lane):
    out = jnp.zeros_like(a)
    for i in range(8):
        line = jnp.sum(jnp.where(lane == row, a[:, i : i + 1], 0.0), axis=0, keepdims=True)
        out = out + jnp.where(row == i, line, 0.0)
    return out


def main_kernel(sizes, dims, rhs, sten, q1_out, q2_out, c_out, p0, q0, pm, pp, w, ws, s0, diag, q2,
                zsend, zrecv, wzsend, wzrecv, red, gacc, gsum, cur, slot_x, slot_y, slot_z, lsem,
                xs, xr, ars, arr):
    nf, nx, ny = dims
    yb_n = ny // 8
    tall = ny + 16
    tiles = tall // 8
    pos = {a: lax.axis_index(a) for a in AXES}
    lane = lax.broadcasted_iota(jnp.int32, (8, 128), 1)
    row = lax.broadcasted_iota(jnp.int32, (8, 128), 0)
    ys = pl.ds(8, ny)

    loads = [
        pltpu.make_async_copy(rhs, p0.at[:, pl.ds(1, nx), ys], lsem.at[0]),
        pltpu.make_async_copy(sten.at[pl.ds(1, 13)], w.at[:, pl.ds(1, nx), ys], lsem.at[1]),
        pltpu.make_async_copy(sten.at[0], s0, lsem.at[2]),
    ]
    for copy in loads:
        copy.start()

    for buf in (p0, q0):
        for x in (0, nx + 1):
            buf[:, x] = jnp.zeros((nf, tall, 128), F32)
    w[:, 0] = jnp.zeros((13, tall, 128), F32)

    def clear(x, carry):
        for y in (0, ny + 8):
            p0[:, x, y : y + 8] = jnp.zeros((nf, 8, 128), F32)
            q0[:, x, y : y + 8] = jnp.zeros((nf, 8, 128), F32)
            w[:, x, y : y + 8] = jnp.zeros((13, 8, 128), F32)
        return carry

    lax.fori_loop(1, nx + 1, clear, 0)
    zrecv[...] = jnp.zeros(zrecv.shape, F32)
    wzrecv[...] = jnp.zeros(wzrecv.shape, F32)

    barrier = pltpu.get_barrier_semaphore()
    for a in AXES:
        for d in range(1, sizes[a]):
            pl.semaphore_signal(barrier, inc=1, device_id={a: lax.rem(pos[a] + d, sizes[a])},
                                device_id_type=pl.DeviceIdType.MESH)
    pl.semaphore_wait(barrier, sum(sizes[a] - 1 for a in AXES))

    count = [0]

    def shift(axis, up, src, dst):
        n = sizes[axis]
        i = pos[axis]
        slot = count[0]
        count[0] += 1
        copy = pltpu.make_async_remote_copy(
            src_ref=src, dst_ref=dst, send_sem=xs.at[slot], recv_sem=xr.at[slot],
            device_id={axis: lax.rem(i + (1 if up else n - 1), n)},
            device_id_type=pl.DeviceIdType.MESH)
        sends = i < n - 1 if up else i > 0
        gets = i > 0 if up else i < n - 1

        @pl.when(sends)
        def _():
            copy.start()

        def finish():
            @pl.when(sends)
            def _():
                copy.wait_send()

            @pl.when(gets)
            def _():
                copy.wait_recv()

        return finish

    def finish_all(items):
        for f in items:
            f()

    def y_faces(buf, start, length):
        xs_ = pl.ds(start, length)
        return [
            shift("gy", True, buf.at[:, xs_, pl.ds(ny, 8)], buf.at[:, xs_, pl.ds(0, 8)]),
            shift("gy", False, buf.at[:, xs_, pl.ds(8, 8)], buf.at[:, xs_, pl.ds(ny + 8, 8)]),
        ]

    def w_faces(start, length, edge):
        xs_ = pl.ds(start, length)
        out = []
        for b, up, src, dst in ((1, True, ny, 0), (-1, False, 8, ny + 8)):
            for lo, hi in runs([k for k, o in enumerate(FORWARD) if o[1] == b and (o[0] or not edge)]):
                ks = pl.ds(lo, hi - lo)
                out.append(shift("gy", up, w.at[ks, xs_, pl.ds(src, 8)], w.at[ks, xs_, pl.ds(dst, 8)]))
        return out

    OWN = (1, nx, 1)
    EDGE = (0, 2, nx + 1)
    W_EDGE = (0, 1, 1)

    def pack(part, take_low, take_high, n_low, n_high):
        first, depth, stride = part

        def body(t, accs):
            low, high = accs
            x = first + t * stride
            for yb in range(tiles):
                j = t * tiles + yb
                here = (lane == j)[None]
                low = jnp.where(here, pltpu.roll(take_low(x, yb), lax.rem(j + 1, 128), 2), low)
                high = jnp.where(here, pltpu.roll(take_high(x, yb), j, 2), high)
            return low, high

        return lax.fori_loop(0, depth, body,
                             (jnp.zeros((n_low, 8, 128), F32), jnp.zeros((n_high, 8, 128), F32)))

    def of(ks):
        def take(x, yb):
            return jnp.concatenate([w[k : k + 1, x, yb * 8 : yb * 8 + 8] for k in ks], axis=0)

        return take

    def gram(g, u, v):
        def body(x, accs):
            accs = list(accs)
            for yb in range(yb_n):
                ub = u(x, yb)
                vb = v(x, yb)
                for i in range(nf):
                    accs[i] = accs[i] + ub[i : i + 1] * vb[i:]
            return tuple(accs)

        accs = lax.fori_loop(0, nx, body, tuple(jnp.zeros((nf - i, 8, 128), F32) for i in range(nf)))
        red[...] = jnp.zeros(red.shape, F32)
        for i in range(nf):
            red[i, i:nf, :] = jnp.sum(accs[i], axis=1)
        out = jnp.zeros((8, 128), F32)
        for i in range(nf):
            t = jnp.sum(red[i], axis=1, keepdims=True)
            out = out + jnp.where(lane == 8 * g + i, t, 0.0)
            line = jnp.sum(jnp.where(lane == 8 * g + row, t, 0.0), axis=0, keepdims=True)
            out = out + jnp.where((row == i) & (lane > 8 * g + i), line, 0.0)
        if g in (0, 3):
            gacc[...] = out
        else:
            gacc[...] += out

    def own(buf):
        return lambda x, yb: buf[:, x + 1, 8 + yb * 8 : 16 + yb * 8]

    def z_send(buf, e, part):
        p = 0 if part is OWN else 1

        def take(x, yb):
            return buf[:, x, yb * 8 : yb * 8 + 8]

        low, high = pack(part, take, take, nf, nf)
        zsend[e, p, 0] = low
        zsend[e, p, 1] = high
        return [
            shift("gz", True, zsend.at[e, p, 0], zrecv.at[e, p, 0]),
            shift("gz", False, zsend.at[e, p, 1], zrecv.at[e, p, 1]),
        ]

    def w_send(part):
        p = 0 if part is OWN else 1
        low, high = pack(part, of(LO), of(HI), len(LO), len(HI))
        wzsend[p, 0 : len(LO)] = low
        wzsend[p, len(LO) : len(LO) + len(HI)] = high
        lo_part, hi_part = pl.ds(0, len(LO)), pl.ds(len(LO), len(HI))
        return [
            shift("gz", True, wzsend.at[p, lo_part], wzrecv.at[p, lo_part]),
            shift("gz", False, wzsend.at[p, hi_part], wzrecv.at[p, hi_part]),
        ]

    def z_fill(buf, e, part):
        p = 0 if part is OWN else 1
        first, depth, stride = part

        def body(t, carry):
            x = first + t * stride
            for yb in range(tiles):
                j = t * tiles + yb
                v = buf[:, x, yb * 8 : yb * 8 + 8]
                low = pltpu.roll(zrecv[e, p, 0], lax.rem(128 - j, 128), 2)
                high = pltpu.roll(zrecv[e, p, 1], 127 - j, 2)
                pm[:, x, yb * 8 : yb * 8 + 8] = jnp.where((lane == 0)[None], low, pltpu.roll(v, 1, 2))
                pp[:, x, yb * 8 : yb * 8 + 8] = jnp.where((lane == 127)[None], high, pltpu.roll(v, 127, 2))
            return carry

        lax.fori_loop(0, depth, body, 0)

    def w_fill(part):
        p = 0 if part is OWN else 1
        first, depth, stride = part

        def body(t, carry):
            x = first + t * stride
            for yb in range(tiles):
                j = t * tiles + yb
                for n, k in enumerate(LO):
                    v = pltpu.roll(w[k, x, yb * 8 : yb * 8 + 8], 1, 1)
                    ws[k, x, yb * 8 : yb * 8 + 8] = jnp.where(
                        lane == 0, pltpu.roll(wzrecv[p, n], lax.rem(128 - j, 128), 1), v)
                for n, k in enumerate(HI):
                    v = pltpu.roll(w[k, x, yb * 8 : yb * 8 + 8], 127, 1)
                    ws[k, x, yb * 8 : yb * 8 + 8] = jnp.where(
                        lane == 127, pltpu.roll(wzrecv[p, len(LO) + n], 127 - j, 1), v)
            return carry

        lax.fori_loop(0, depth, body, 0)

    def behind(k, x, yb):
        a, b, c = FORWARD[k]
        src = w if c == 0 else ws
        return src[k, x + 1 - a, 8 + yb * 8 - b : 16 + yb * 8 - b]

    def ahead(k, x, yb):
        return w[k, x + 1, 8 + yb * 8 : 16 + yb * 8]

    def stencil(buf, put, first, depth, stride):
        views = {0: buf, -1: pm, 1: pp}

        def body(t, carry):
            x = first + t * stride
            for yb in range(yb_n):
                y = 8 + yb * 8
                acc = diag[x, yb * 8 : yb * 8 + 8][None] * buf[:, x + 1, y : y + 8]
                for k, (a, b, c) in enumerate(FORWARD):
                    acc = acc - ahead(k, x, yb)[None] * views[c][:, x + 1 + a, y + b : y + b + 8]
                    acc = acc - behind(k, x, yb)[None] * views[-c][:, x + 1 - a, y - b : y - b + 8]
                put(x, yb, acc)
            return carry

        lax.fori_loop(0, depth, body, 0)

    all_slots = (slot_y, slot_x, slot_z)
    bases = [0]
    for a in ("gy", "gx"):
        bases.append(bases[-1] + sizes[a] - 1)

    def sum_start(r, stage, value):
        a = ("gy", "gx", "gz")[stage]
        slots = all_slots[stage]
        n = sizes[a]
        i = pos[a]
        cur[r, stage] = value
        slots[r, i] = value

        def copy(d, dst):
            m = bases[stage] + d - 1
            return pltpu.make_async_remote_copy(
                src_ref=cur.at[r, stage], dst_ref=slots.at[r, dst],
                send_sem=ars.at[r, m], recv_sem=arr.at[r, m],
                device_id={a: lax.rem(i + d, n)}, device_id_type=pl.DeviceIdType.MESH)

        for d in range(1, n):
            copy(d, i).start()

        def finish():
            for d in range(1, n):
                copy(d, i).wait_send()
                copy(d, lax.rem(i + n - d, n)).wait_recv()
            total = slots[r, 0]
            for q in range(1, n):
                total = total + slots[r, q]
            return total

        return finish

    k0, k1 = EX[0], EX[-1] + 1
    phase = [
        shift("gx", True, rhs.at[:, nx - 1], p0.at[:, 0, ys]),
        shift("gx", False, rhs.at[:, 0], p0.at[:, nx + 1, ys]),
        shift("gx", True, sten.at[pl.ds(k0 + 1, k1 - k0), nx - 1], w.at[pl.ds(k0, k1 - k0), 0, ys]),
    ]
    def make_diag(x, carry):
        for yb in range(yb_n):
            total = s0[x, yb * 8 : yb * 8 + 8]
            for k in range(13):
                total = total + ahead(k, x, yb) + behind(k, x, yb)
            diag[x, yb * 8 : yb * 8 + 8] = total
        return carry

    def put_q1(x, yb, v):
        q0[:, x + 1, 8 + yb * 8 : 16 + yb * 8] = v

    def put_q2(x, yb, v):
        q2[:, x, yb * 8 : yb * 8 + 8] = v

    def stencil_pairs(buf, put, first, pairs):
        views = {0: buf, -1: pm, 1: pp}

        def body(t, carry):
            x = first + 2 * t
            for yb in range(yb_n):
                y = 8 + yb * 8
                accs = [None, None]
                for dx in (-1, 0, 1, 2):
                    for dy in (-1, 0, 1):
                        for dz in (-1, 0, 1):
                            v = views[dz][:, x + 1 + dx, y + dy : y + dy + 8]
                            for plane in (0, 1):
                                o = (dx - plane, dy, dz)
                                if abs(o[0]) > 1:
                                    continue
                                if o == (0, 0, 0):
                                    coef = -diag[x + plane, yb * 8 : yb * 8 + 8]
                                elif o > (0, 0, 0):
                                    coef = ahead(FORWARD.index(o), x + plane, yb)
                                else:
                                    back = (-o[0], -o[1], -o[2])
                                    coef = behind(FORWARD.index(back), x + plane, yb)
                                term = coef[None] * v
                                accs[plane] = -term if accs[plane] is None else accs[plane] - term
                for plane in (0, 1):
                    put(x + plane, yb, accs[plane])
            return carry

        lax.fori_loop(0, pairs, body, 0)

    half = (nx - 2) // 4

    def operate(buf, e, put, crossing, hooks=()):
        finish_all(crossing)
        ends = y_faces(buf, 0, 1) + y_faces(buf, nx + 1, 1)
        if e == 0:
            ends += w_faces(0, 1, True)
        stencil_pairs(buf, put, 1, half)
        if hooks:
            hooks[0]()
        finish_all(ends)
        ends = z_send(buf, e, EDGE)
        if e == 0:
            ends += w_send(W_EDGE)
        stencil_pairs(buf, put, 1 + 2 * half, (nx - 2) // 2 - half)
        if hooks:
            hooks[1]()
        finish_all(ends)
        z_fill(buf, e, EDGE)
        if e == 0:
            w_fill(W_EDGE)
            lax.fori_loop(0, 1, make_diag, 0)
        stencil(buf, put, 0, 2, nx - 1)

    loads[0].wait()
    sides = y_faces(p0, 1, nx)
    loads[1].wait()
    sides += w_faces(1, nx, False)
    gram(0, own(p0), own(p0))
    loads[2].wait()
    finish_all(sides)
    sides = z_send(p0, 0, OWN)
    sides += w_send(OWN)
    finish_all(sides)
    z_fill(p0, 0, OWN)
    w_fill(OWN)
    lax.fori_loop(1, nx, make_diag, 0)
    operate(p0, 0, put_q1, phase)

    sides = y_faces(q0, 1, nx)
    phase = [
        shift("gx", True, q0.at[:, nx, ys], q0.at[:, 0, ys]),
        shift("gx", False, q0.at[:, 1, ys], q0.at[:, nx + 1, ys]),
    ]
    save1 = pltpu.make_async_copy(q0.at[:, pl.ds(1, nx), ys], q1_out, lsem.at[3])
    save1.start()
    gram(1, own(p0), own(q0))
    finish_all(sides)
    sides = z_send(q0, 1, OWN)
    gram(2, own(q0), own(q0))
    pending = [sum_start(0, 0, gacc[...])]
    finish_all(sides)
    z_fill(q0, 1, OWN)
    pending.append(sum_start(0, 1, pending[0]()))

    def hook_a():
        pending.append(sum_start(0, 2, pending[1]()))

    def hook_b():
        gsum[...] = pending[2]()

    operate(q0, 1, put_q2, phase, (hook_a, hook_b))
    save2 = pltpu.make_async_copy(q2, q2_out, lsem.at[4])
    save2.start()
    gram(3, own(q0), lambda x, yb: q2[:, x, yb * 8 : yb * 8 + 8])

    done = sum_start(1, 0, gacc[...])
    total = gsum[...]
    small = lane < 8
    parts = [jnp.where(small, pltpu.roll(total, (128 - 8 * g) % 128, 1), 0.0) for g in range(3)]
    rr, pq, ss = parts
    alpha = jnp.where(small, solve(pq, rr, row), 0.0)
    done = sum_start(1, 1, done())
    alpha_t = transposed(alpha, row, lane)
    alpha_t = jnp.where(small, alpha_t, 0.0)
    ssa = mm(ss, alpha)
    new = rr - mm(alpha_t, pq) - mm(pq, alpha) + mm(alpha_t, ssa)
    beta = jnp.where(small, solve(rr, new, row), 0.0)
    done = sum_start(1, 2, done())
    ib = beta + jnp.where(lane == row, 1.0, 0.0)
    ib_t = jnp.where(small, transposed(ib, row, lane), 0.0)
    left = mm(ib_t, mm(pq, ib) - ssa)
    mid = mm(ss, ib)
    tt = jnp.where(small, pltpu.roll(done(), 128 - 24, 1), 0.0)
    curve = left - mm(alpha_t, mid - mm(tt, alpha))
    alpha1 = jnp.where(small, solve(curve, new, row), 0.0)
    c_out[0] = alpha + mm(ib, alpha1)
    c_out[1] = mm(alpha, alpha1)
    save1.wait()
    save2.wait()


def final_kernel(yb_n, xs_n, c, r0, q1, q2, sol, res, table):
    @pl.when(pl.program_id(0) == 0)
    def _():
        for n in range(2):
            for i in range(8):
                for j in range(8):
                    table[n, i, j] = jnp.full((8, 128), c[n, i, j], F32)

    def body(x, carry):
        for yb in range(yb_n):
            y = slice(yb * 8, yb * 8 + 8)
            s = jnp.zeros((8, 8, 128), F32)
            e = r0[:, x, y]
            for i in range(8):
                t1, t2 = table[0, i], table[1, i]
                a, b, d = r0[i, x, y][None], q1[i, x, y][None], q2[i, x, y][None]
                s = s + (t1 * a - t2 * b)
                e = e + (t2 * d - t1 * b)
            sol[:, x, y] = s
            res[:, x, y] = e
        return carry

    lax.fori_loop(0, xs_n, body, 0)


def shards(sizes, rhs, stencil):
    nf, nx, ny, nz = rhs.shape
    tall = ny + 16
    field = jax.ShapeDtypeStruct(rhs.shape, F32)
    anyspace = pl.BlockSpec(memory_space=pl.ANY)
    peers = sum(sizes[a] - 1 for a in AXES)
    padded = pltpu.VMEM((nf, nx + 2, tall, nz), F32)

    def kernel(*refs):
        main_kernel(sizes, (nf, nx, ny), *refs)

    q1, q2, c = pl.pallas_call(
        kernel,
        out_shape=(field, field, jax.ShapeDtypeStruct((2, 8, 128), F32)),
        in_specs=[anyspace, anyspace],
        out_specs=(anyspace, anyspace, pl.BlockSpec(memory_space=pltpu.VMEM)),
        scratch_shapes=[
            padded, padded, padded, padded,
            pltpu.VMEM((13, nx + 1, tall, nz), F32),
            pltpu.VMEM((13, nx + 1, tall, nz), F32),
            pltpu.VMEM((nx, ny, nz), F32),
            pltpu.VMEM((nx, ny, nz), F32),
            pltpu.VMEM((nf, nx, ny, nz), F32),
            pltpu.VMEM((2, 2, 2, nf, 8, nz), F32),
            pltpu.VMEM((2, 2, 2, nf, 8, nz), F32),
            pltpu.VMEM((2, len(LO) + len(HI), 8, nz), F32),
            pltpu.VMEM((2, len(LO) + len(HI), 8, nz), F32),
            pltpu.VMEM((8, 8, 128), F32),
            pltpu.VMEM((8, 128), F32),
            pltpu.VMEM((8, 128), F32),
            pltpu.VMEM((2, 3, 8, 128), F32),
            pltpu.VMEM((2, sizes["gx"], 8, 128), F32),
            pltpu.VMEM((2, sizes["gy"], 8, 128), F32),
            pltpu.VMEM((2, sizes["gz"], 8, 128), F32),
            pltpu.SemaphoreType.DMA((5,)),
            pltpu.SemaphoreType.DMA((40,)),
            pltpu.SemaphoreType.DMA((40,)),
            pltpu.SemaphoreType.DMA((2, peers)),
            pltpu.SemaphoreType.DMA((2, peers)),
        ],
        compiler_params=pltpu.CompilerParams(
            collective_id=0, has_side_effects=True, vmem_limit_bytes=60 * 2**20),
        name="krylov",
    )(rhs, stencil)

    step = 2
    block = pl.BlockSpec((nf, step, ny, nz), lambda i: (0, i, 0, 0))

    def last(*refs):
        final_kernel(ny // 8, step, *refs)

    return pl.pallas_call(
        last,
        grid=(nx // step,),
        out_shape=(field, field),
        in_specs=[pl.BlockSpec(memory_space=pltpu.SMEM), block, block, block],
        out_specs=(block, block),
        scratch_shapes=[pltpu.VMEM((2, 8, 8, 8, 128), F32)],
        compiler_params=pltpu.CompilerParams(dimension_semantics=("arbitrary",), vmem_limit_bytes=60 * 2**20),
        name="combine",
    )(c, rhs, q1, q2)


def solution(mesh):
    sizes = {a: mesh.shape[a] for a in AXES}
    spec = P(None, "gx", "gy", "gz")

    def run(rhs, stencil):
        return shards(sizes, rhs, stencil)

    return jax.shard_map(run, mesh=mesh, in_specs=(spec, spec), out_specs=(spec, spec), check_vma=False)
```

profile of v0, /device:TPU:0, one launch (start us, length us, event | category | flops | bytes accessed | tf_op | source)
XLA Modules:
  0.0 71.4 jit_solution(12013788215581858945)
XLA Ops:
  0.6 61.5 %krylov.1 = (f32[8,16,32,128]{3,2,1,0:T(8,128)}, f32[8,16,32,128]{3,2,1,0:T(8,128)}, f32[2,8,128]{2,1,0:T(8,128)}) custom-call(f32[8,16,32,128]{3,2,1,0:T(8,128)} %refs_1_.3, f32[14,16,32,128]{3,2,1,0:T(8,128)} %refs_1_.2), custom_call_target="tpu_custom_call" | custom-call | tf_op jit(solution)/shard_map/krylov/pallas_call | solution.py:496
  62.1 9.2 %combine.1 = (f32[8,16,32,128]{3,2,1,0:T(8,128)}, f32[8,16,32,128]{3,2,1,0:T(8,128)}) custom-call(f32[2,8,128]{2,1,0:T(8,128)} %get-tuple-element.5.refs_0_, f32[8,16,32,128]{3,2,1,0:T(8,128)} %refs_1_.3, f32[8,16,32,128]{3,2,1,0:T(8,128)} %get-tuple-element.6.refs_2_, f32[8,16,32,128]{3,2,1,0:T(8,128)} %get-tuple-element.7.refs_3_), custom_call_target="tpu_custom_call" | custom-call | tf_op jit(solution)/shard_map/combine/pallas_call | solution.py:536
where the time goes:
time: 71.7 us; the launch traced here: 71.4 us
  Pallas kernels  70.7 us (99%)
    pallas_call x1, Pallas kernels, shards(): pl.pallas_call(kernel, out_shape=(field, field, jax.ShapeDtypeStruct((2,...  61.5 us
    pallas_call x1, Pallas kernels, shards(): pl.pallas_call(last, grid=(nx // step,), out_shape=(field, field), in_spe...  9.23 us

commit v1 on v0

v1 whole, which is shorter than its diff:
```python
import jax
import jax.numpy as jnp
from jax import lax
from jax.experimental import pallas as pl
from jax.experimental.pallas import tpu as pltpu
from jax.sharding import PartitionSpec as P

FORWARD = [
    (a, b, c) for a in (-1, 0, 1) for b in (-1, 0, 1) for c in (-1, 0, 1) if (a, b, c) > (0, 0, 0)
]
AXES = ("gx", "gy", "gz")
LO = [k for k, o in enumerate(FORWARD) if o[2] == 1]
HI = [k for k, o in enumerate(FORWARD) if o[2] == -1]
EX = [k for k, o in enumerate(FORWARD) if o[0] == 1]
F32 = jnp.float32
NS = jax.named_scope


def runs(ks):
    out = []
    for k in ks:
        if out and out[-1][1] == k:
            out[-1][1] = k + 1
        else:
            out.append([k, k + 1])
    return out


def splat(a, k):
    return jnp.broadcast_to(a[:, k : k + 1], (8, 128))


def line(a, k):
    return jnp.broadcast_to(a[k : k + 1, :], (8, 128))


def columns(a):
    return [splat(a, k) for k in range(8)]


def mm(cols, b):
    parts = [cols[k] * line(b, k) for k in range(8)]
    while len(parts) > 1:
        parts = [parts[i] + parts[i + 1] for i in range(0, len(parts), 2)]
    return parts[0]


def solve(cols, b, row):
    cols = list(cols)
    for k in range(8):
        factor = cols[k]
        inverse = 1.0 / line(factor, k)
        pivot = line(b, k) * inverse
        b = jnp.where(row == k, pivot, b - factor * pivot)
        for j in range(k + 1, 8):
            pivot = line(cols[j], k) * inverse
            cols[j] = jnp.where(row == k, pivot, cols[j] - factor * pivot)
    return b


def transposed(a, row, lane):
    out = jnp.zeros_like(a)
    for i in range(8):
        across = jnp.sum(jnp.where(lane == row, a[:, i : i + 1], 0.0), axis=0, keepdims=True)
        out = out + jnp.where(row == i, across, 0.0)
    return out


def main_kernel(sizes, dims, rhs, sten, q1_out, q2_out, c_out, p0, q0, w, ws, s0, diag, q2, scr,
                zsend, zrecv, esend, erecv, wzsend, wzrecv, ufull, uedge, uw, red, gacc, gsum, cur,
                slot_x, slot_y, slot_z, lsem, xs, xr, ars, arr):
    nf, nx, ny = dims
    yb_n = ny // 8
    tall = ny + 16
    per = 4 * yb_n
    pos = {a: lax.axis_index(a) for a in AXES}
    lane = lax.broadcasted_iota(jnp.int32, (8, 128), 1)
    row = lax.broadcasted_iota(jnp.int32, (8, 128), 0)
    first_lane = lane == 0
    last_lane = lane == 127
    rim = first_lane | last_lane
    even = lax.rem(lane, 2) == 0
    half_lane = lane // 2
    ys = pl.ds(8, ny)
    SHIFTED = LO + HI

    barrier = pltpu.get_barrier_semaphore()
    for a in AXES:
        for d in range(1, sizes[a]):
            pl.semaphore_signal(barrier, inc=1, device_id={a: lax.rem(pos[a] + d, sizes[a])},
                                device_id_type=pl.DeviceIdType.MESH)

    loads = [
        pltpu.make_async_copy(rhs, p0.at[:, pl.ds(1, nx), ys], lsem.at[0]),
        pltpu.make_async_copy(sten.at[pl.ds(1, 13)], w.at[:, pl.ds(1, nx), ys], lsem.at[1]),
        pltpu.make_async_copy(sten.at[0], s0, lsem.at[2]),
    ]
    for copy in loads:
        copy.start()

    last = {a: sizes[a] - 1 for a in AXES}

    @pl.when(pos["gx"] == 0)
    def _():
        for buf in (p0, q0):
            buf[:, 0, ys] = jnp.zeros((nf, ny, 128), F32)
        w[:, 0, ys] = jnp.zeros((13, ny, 128), F32)

    @pl.when(pos["gx"] == last["gx"])
    def _():
        for buf in (p0, q0):
            buf[:, nx + 1, ys] = jnp.zeros((nf, ny, 128), F32)

    def clear_y(y):
        def body(x, carry):
            for buf in (p0, q0):
                buf[:, x, y : y + 8] = jnp.zeros((nf, 8, 128), F32)
            return carry

        lax.fori_loop(0, nx + 2, body, 0)

        def body_w(x, carry):
            w[:, x, y : y + 8] = jnp.zeros((13, 8, 128), F32)
            return carry

        lax.fori_loop(0, nx + 1, body_w, 0)

    @pl.when(pos["gy"] == 0)
    def _():
        clear_y(0)

    @pl.when(pos["gy"] == last["gy"])
    def _():
        clear_y(ny + 8)

    for side, place in ((0, 0), (1, last["gz"])):
        @pl.when(pos["gz"] == place)
        def _():
            for e in range(2):
                zrecv[e, side] = jnp.zeros((nf + 1, 8, 128), F32)
                erecv[e, side] = jnp.zeros((2, 8, 128), F32)
            wzrecv[side] = jnp.zeros((len(LO), 8, 128), F32)

    zsend[...] = jnp.zeros(zsend.shape, F32)
    esend[...] = jnp.zeros(esend.shape, F32)
    wzsend[...] = jnp.zeros(wzsend.shape, F32)

    pl.semaphore_wait(barrier, sum(sizes[a] - 1 for a in AXES))

    count = [0]

    def shift(axis, up, src, dst):
        n = sizes[axis]
        i = pos[axis]
        slot = count[0]
        count[0] += 1
        copy = pltpu.make_async_remote_copy(
            src_ref=src, dst_ref=dst, send_sem=xs.at[slot], recv_sem=xr.at[slot],
            device_id={axis: lax.rem(i + (1 if up else n - 1), n)},
            device_id_type=pl.DeviceIdType.MESH)
        sends = i < n - 1 if up else i > 0
        gets = i > 0 if up else i < n - 1

        @pl.when(sends)
        def _():
            copy.start()

        def finish():
            @pl.when(sends)
            def _():
                copy.wait_send()

            @pl.when(gets)
            def _():
                copy.wait_recv()

        return finish

    def finish_all(items):
        for f in items:
            f()

    def y_faces(buf, start, length):
        xs_ = pl.ds(start, length)
        return [
            shift("gy", True, buf.at[:, xs_, pl.ds(ny, 8)], buf.at[:, xs_, pl.ds(0, 8)]),
            shift("gy", False, buf.at[:, xs_, pl.ds(8, 8)], buf.at[:, xs_, pl.ds(ny + 8, 8)]),
        ]

    def w_faces(start, length, edge):
        xs_ = pl.ds(start, length)
        out = []
        for b, up, src, dst in ((1, True, ny, 0), (-1, False, 8, ny + 8)):
            for lo, hi in runs([k for k, o in enumerate(FORWARD) if o[1] == b and (o[0] or not edge)]):
                ks = pl.ds(lo, hi - lo)
                out.append(shift("gy", up, w.at[ks, xs_, pl.ds(src, 8)], w.at[ks, xs_, pl.ds(dst, 8)]))
        return out

    def x_faces(buf):
        return [
            shift("gx", True, buf.at[:, nx, ys], buf.at[:, 0, ys]),
            shift("gx", False, buf.at[:, 1, ys], buf.at[:, nx + 1, ys]),
        ]

    def z_both(send, recv):
        return [
            shift("gz", True, send, recv.at[0]),
            shift("gz", False, send, recv.at[1]),
        ]

    def gram_body(accs, ub, vb):
        return [accs[i] + ub[i : i + 1] * vb[i:] for i in range(nf)]

    def gram_start():
        return tuple(jnp.zeros((nf - i, 8, 128), F32) for i in range(nf))

    def gram_end(g, accs):
        red[...] = jnp.zeros(red.shape, F32)
        for i in range(nf):
            red[i, i:nf, :] = jnp.sum(accs[i], axis=1)
        out = jnp.zeros((8, 128), F32)
        for i in range(nf):
            t = jnp.sum(red[i], axis=1, keepdims=True)
            out = out + jnp.where(lane == 8 * g + i, t, 0.0)
            across = jnp.sum(jnp.where(lane == 8 * g + row, t, 0.0), axis=0, keepdims=True)
            out = out + jnp.where((row == i) & (lane > 8 * g + i), across, 0.0)
        if g in (0, 3):
            gacc[...] = out
        else:
            gacc[...] += out

    def own(buf):
        return lambda x, yb: buf[:, x + 1, 8 + yb * 8 : 16 + yb * 8]

    def gram_plane(accs, u, v, x):
        for yb in range(yb_n):
            accs = gram_body(accs, u(x, yb), v(x, yb))
        return tuple(accs)

    def gram(g, u, v):
        gram_end(g, lax.fori_loop(0, nx, lambda x, accs: gram_plane(accs, u, v, x), gram_start()))

    def pack_w(x, carry):
        for yb in range(yb_n):
            j = x * yb_n + yb
            here = half_lane == j
            y = 8 + yb * 8
            for n, k in enumerate(LO):
                both = w[k, x + 1, y : y + 8]
                if n < len(HI):
                    both = jnp.where(first_lane, w[HI[n], x + 1, y : y + 8], both)
                pltpu.store(wzsend.at[n], pltpu.roll(both, 2 * j + 1, 1), mask=here)
        return carry

    def shift_w(x, carry):
        for yb in range(yb_n):
            y = 8 + yb * 8
            for n, k in enumerate(SHIFTED):
                ws[n, x, yb * 8 : yb * 8 + 8] = pltpu.roll(w[k, x + 1, y : y + 8], 1 if k in LO else 127, 1)
        return carry

    def insert_w(x, carry):
        for yb in range(yb_n):
            j = x * yb_n + yb
            for n in range(len(LO)):
                edge = pltpu.roll(uw[n], 127 - 2 * j, 1)
                pltpu.store(ws.at[n, x, yb * 8 : yb * 8 + 8], edge, mask=first_lane)
                if n < len(HI):
                    pltpu.store(ws.at[len(LO) + n, x, yb * 8 : yb * 8 + 8], edge, mask=last_lane)
        return carry

    def crossing(from_low, from_high):
        return jnp.where(even, pltpu.roll(from_high, 127, 1), pltpu.roll(from_low, 1, 1))

    def sums(buf, e, x):
        for yb in range(yb_n):
            y = 8 + yb * 8
            accs = {}
            back = {}
            for a in (-1, 0, 1):
                for b in (-1, 0, 1):
                    v = buf[:, x + 1 + a, y + b : y + b + 8]
                    for c in (-1, 0, 1):
                        o = (a, b, c)
                        if o == (0, 0, 0):
                            continue
                        if o > (0, 0, 0):
                            k = FORWARD.index(o)
                            if c == 0:
                                coef = w[k, x + 1, y : y + 8]
                            else:
                                coef = ws[SHIFTED.index(k), x, yb * 8 : yb * 8 + 8]
                        else:
                            k = FORWARD.index((-a, -b, -c))
                            coef = w[k, x + 1 + a, y + b : y + b + 8]
                            if e == 0:
                                back[c] = coef if c not in back else back[c] + coef
                        term = coef[None] * v
                        accs[c] = term if c not in accs else accs[c] + term
            if e == 0:
                total = s0[x, yb * 8 : yb * 8 + 8] + back[0]
                for k in range(13):
                    total = total + w[k, x + 1, y : y + 8]
                back[0] = total
            for c in (-1, 0, 1):
                scr[c + 1, yb, 0:nf] = accs[c]
                if e == 0:
                    scr[c + 1, yb, nf] = back[c]

    def settle(buf, e, x, put, where):
        for yb in range(yb_n):
            y = 8 + yb * 8
            j = x * yb_n + yb
            if where is None:
                here = half_lane == j
            if e == 0:
                up, down = scr[2, yb, nf], scr[0, yb, nf]
                total = scr[1, yb, nf] + pltpu.roll(up, 127, 1) + pltpu.roll(down, 1, 1)
                diag[x, yb * 8 : yb * 8 + 8] = total
                both = jnp.where(first_lane, up, down)
                if where is None:
                    pltpu.store(zsend.at[e, nf], pltpu.roll(both, 2 * j + 1, 1), mask=here)
                else:
                    m = where * yb_n + yb
                    pltpu.store(esend.at[e, 1], pltpu.roll(both, 2 * m + 1, 1), mask=half_lane == m)
            else:
                total = diag[x, yb * 8 : yb * 8 + 8]
            for f in range(nf):
                up, down = scr[2, yb, f], scr[0, yb, f]
                total_f = scr[1, yb, f] + pltpu.roll(up, 127, 1) + pltpu.roll(down, 1, 1)
                put(f, x, yb, total * buf[f, x + 1, y : y + 8] - total_f)
                both = jnp.where(first_lane, up, down)
                if where is None:
                    pltpu.store(zsend.at[e, f], pltpu.roll(both, 2 * j + 1, 1), mask=here)
                else:
                    m = f * (per // 2) + where * yb_n + yb
                    pltpu.store(esend.at[e, 0], pltpu.roll(both, (2 * m + 1) % 128, 1), mask=half_lane == m)

    def gather_full(e):
        for f in range(nf + 1 - e):
            mine = zsend[e, f]
            ufull[f] = crossing(zrecv[e, 0, f] - mine, zrecv[e, 1, f] - mine)

    def gather_edge(e):
        for n in range(2 - e):
            mine = esend[e, n]
            uedge[n] = crossing(erecv[e, 0, n] - mine, erecv[e, 1, n] - mine)

    def mend(buf, e, x, get, put, where):
        for yb in range(yb_n):
            y = 8 + yb * 8
            j = x * yb_n + yb
            if e == 0:
                if where is None:
                    extra = pltpu.roll(ufull[nf], 127 - 2 * j, 1)
                else:
                    extra = pltpu.roll(uedge[1], 127 - 2 * (where * yb_n + yb), 1)
                extra = jnp.where(rim, extra, 0.0)
                diag[x, yb * 8 : yb * 8 + 8] += extra
            for f in range(nf):
                if where is None:
                    edge = pltpu.roll(ufull[f], 127 - 2 * j, 1)
                else:
                    edge = pltpu.roll(uedge[0], 127 - 2 * (f * (per // 2) + where * yb_n + yb), 1)
                value = get(f, x, yb) - jnp.where(rim, edge, 0.0)
                if e == 0:
                    value = value + extra * buf[f, x + 1, y : y + 8]
                put(f, x, yb, value)

    all_slots = (slot_y, slot_x, slot_z)
    bases = [0]
    for a in ("gy", "gx"):
        bases.append(bases[-1] + sizes[a] - 1)

    def sum_start(r, stage, value):
        a = ("gy", "gx", "gz")[stage]
        slots = all_slots[stage]
        n = sizes[a]
        i = pos[a]
        cur[r, stage] = value
        slots[r, i] = value

        def copy(d, dst):
            m = bases[stage] + d - 1
            return pltpu.make_async_remote_copy(
                src_ref=cur.at[r, stage], dst_ref=slots.at[r, dst],
                send_sem=ars.at[r, m], recv_sem=arr.at[r, m],
                device_id={a: lax.rem(i + d, n)}, device_id_type=pl.DeviceIdType.MESH)

        for d in range(1, n):
            copy(d, i).start()

        def finish():
            for d in range(1, n):
                copy(d, i).wait_send()
                copy(d, lax.rem(i + n - d, n)).wait_recv()
            total = slots[r, 0]
            for q in range(1, n):
                total = total + slots[r, q]
            return total

        return finish

    k0, k1 = EX[0], EX[-1] + 1

    def put_q1(f, x, yb, v):
        q0[f, x + 1, 8 + yb * 8 : 16 + yb * 8] = v

    def get_q1(f, x, yb):
        return q0[f, x + 1, 8 + yb * 8 : 16 + yb * 8]

    def put_q2(f, x, yb, v):
        q2[f, x, yb * 8 : yb * 8 + 8] = v

    def get_q2(f, x, yb):
        return q2[f, x, yb * 8 : yb * 8 + 8]

    half = nx // 2

    def planes(buf, e, put, lo, hi):
        def body(x, carry):
            settle(buf, e, x - 1, put, None)
            sums(buf, e, x)
            return carry

        lax.fori_loop(lo, hi, body, 0)

    def operate(buf, e, put, across, hooks=()):
        with NS(f"op{e}_st1"):
            sums(buf, e, 1)
            planes(buf, e, put, 2, half)
        with NS(f"op{e}_xwait"):
            finish_all(across)
            ends = y_faces(buf, 0, 1) + y_faces(buf, nx + 1, 1)
            if e == 0:
                ends += w_faces(0, 1, True)
        if hooks:
            hooks[0]()
        with NS(f"op{e}_st2"):
            planes(buf, e, put, half, nx - 1)
        with NS(f"op{e}_ywait"):
            finish_all(ends)
        if hooks:
            hooks[1]()
        with NS(f"op{e}_st3"):
            settle(buf, e, nx - 2, put, None)
            sums(buf, e, 0)
            first = z_both(zsend.at[e, pl.ds(0, nf + 1 - e)], zrecv.at[e, :, pl.ds(0, nf + 1 - e)])
            settle(buf, e, 0, put, 0)
            sums(buf, e, nx - 1)
            settle(buf, e, nx - 1, put, 1)
            second = z_both(esend.at[e, pl.ds(0, 2 - e)], erecv.at[e, :, pl.ds(0, 2 - e)])
        return first, second

    with NS("a_load"):
        loads[0].wait()
        sides = y_faces(p0, 1, nx)
        phase = x_faces(p0)
        loads[1].wait()
        sides += w_faces(1, nx, False)
        phase.append(shift("gx", True, w.at[pl.ds(k0, k1 - k0), nx, ys], w.at[pl.ds(k0, k1 - k0), 0, ys]))
    with NS("a_packw"):
        lax.fori_loop(0, nx, pack_w, 0)
        zw = z_both(wzsend, wzrecv)
    with NS("a_gram0"):
        gram(0, own(p0), own(p0))
    with NS("a_shiftw"):
        lax.fori_loop(0, nx, shift_w, 0)
    with NS("a_zwait"):
        finish_all(zw)
    with NS("a_insw"):
        for n in range(len(LO)):
            uw[n] = crossing(wzrecv[0, n], wzrecv[1, n])
        lax.fori_loop(0, nx, insert_w, 0)
    with NS("a_ywait"):
        loads[2].wait()
        finish_all(sides)
    first, second = operate(p0, 0, put_q1, phase)

    def mend_gram(buf, e, get, put, u, v, accs):
        mend(buf, e, 1, get, put, None)

        def body(x, accs):
            accs = gram_plane(accs, u, v, x)
            mend(buf, e, x + 1, get, put, None)
            return accs

        return gram_plane(lax.fori_loop(1, nx - 2, body, accs), u, v, nx - 2)

    with NS("b_zwait1"):
        finish_all(first)
        gather_full(0)
    with NS("b_mend"):
        accs = mend_gram(p0, 0, get_q1, put_q1, own(p0), own(q0), gram_start())
    with NS("b_zwait2"):
        finish_all(second)
    with NS("b_mend2"):
        gather_edge(0)
        mend(p0, 0, 0, get_q1, put_q1, 0)
        mend(p0, 0, nx - 1, get_q1, put_q1, 1)
        phase = x_faces(q0)
        sides = y_faces(q0, 1, nx)
        save1 = pltpu.make_async_copy(q0.at[:, pl.ds(1, nx), ys], q1_out, lsem.at[3])
        save1.start()
    with NS("b_gram1"):
        accs = gram_plane(accs, own(p0), own(q0), 0)
        accs = gram_plane(accs, own(p0), own(q0), nx - 1)
        gram_end(1, accs)
    with NS("b_gram2"):
        gram(2, own(q0), own(q0))
        pending = [sum_start(0, 0, gacc[...])]
    with NS("b_ywait"):
        finish_all(sides)
        pending.append(sum_start(0, 1, pending[0]()))

    def hook_a():
        with NS("hook_a"):
            pending.append(sum_start(0, 2, pending[1]()))

    def hook_b():
        with NS("hook_b"):
            gsum[...] = pending[2]()

    first, second = operate(q0, 1, put_q2, phase, (hook_a, hook_b))

    def get_v2(x, yb):
        return q2[:, x, yb * 8 : yb * 8 + 8]

    with NS("c_zwait1"):
        finish_all(first)
        gather_full(1)
    with NS("c_mend"):
        accs = mend_gram(q0, 1, get_q2, put_q2, own(q0), get_v2, gram_start())

    with NS("c_alg1"):
        total = gsum[...]
        small = lane < 8
        rr, pq, ss = [jnp.where(small, pltpu.roll(total, (128 - 8 * g) % 128, 1), 0.0) for g in range(3)]
        pqc, rrc, ssc = columns(pq), columns(rr), columns(ss)
        alpha = jnp.where(small, solve(pqc, rr, row), 0.0)
        alpha_t = jnp.where(small, transposed(alpha, row, lane), 0.0)
        alpha_c, alpha_tc = columns(alpha), columns(alpha_t)
        ssa = mm(ssc, alpha)
        new = rr - mm(alpha_tc, pq) - mm(pqc, alpha) + mm(alpha_tc, ssa)
        beta = jnp.where(small, solve(rrc, new, row), 0.0)
        ib = beta + jnp.where(lane == row, 1.0, 0.0)
        ib_t = jnp.where(small, transposed(ib, row, lane), 0.0)
        left = mm(columns(ib_t), mm(pqc, ib) - ssa)
        mid = mm(ssc, ib)
        left = left - mm(alpha_tc, mid)
    with NS("c_zwait2"):
        finish_all(second)
    with NS("c_mend2"):
        gather_edge(1)
        mend(q0, 1, 0, get_q2, put_q2, 0)
        mend(q0, 1, nx - 1, get_q2, put_q2, 1)
        save2 = pltpu.make_async_copy(q2, q2_out, lsem.at[4])
        save2.start()
        accs = gram_plane(accs, own(q0), get_v2, 0)
        accs = gram_plane(accs, own(q0), get_v2, nx - 1)
        gram_end(3, accs)
    with NS("c_sum"):
        done = sum_start(1, 0, gacc[...])
        done = sum_start(1, 1, done())
        done = sum_start(1, 2, done())
        total = done()
    with NS("c_alg2"):
        tt = jnp.where(small, pltpu.roll(total, 128 - 24, 1), 0.0)
        curve = left + mm(alpha_tc, mm(columns(tt), alpha))
        alpha1 = jnp.where(small, solve(columns(curve), new, row), 0.0)
        c_out[0] = alpha + mm(columns(ib), alpha1)
        c_out[1] = mm(alpha_c, alpha1)
    with NS("c_end"):
        save1.wait()
        save2.wait()


def final_kernel(yb_n, xs_n, c, r0, q1, q2, sol, res, table):
    @pl.when(pl.program_id(0) == 0)
    def _():
        for n in range(2):
            for i in range(8):
                for j in range(8):
                    table[n, i, j] = jnp.full((8, 128), c[n, i, j], F32)

    def body(x, carry):
        for yb in range(yb_n):
            y = slice(yb * 8, yb * 8 + 8)
            s = jnp.zeros((8, 8, 128), F32)
            e = r0[:, x, y]
            for i in range(8):
                t1, t2 = table[0, i], table[1, i]
                a, b, d = r0[i, x, y][None], q1[i, x, y][None], q2[i, x, y][None]
                s = s + (t1 * a - t2 * b)
                e = e + (t2 * d - t1 * b)
            sol[:, x, y] = s
            res[:, x, y] = e
        return carry

    lax.fori_loop(0, xs_n, body, 0)


def shards(sizes, rhs, stencil):
    nf, nx, ny, nz = rhs.shape
    tall = ny + 16
    field = jax.ShapeDtypeStruct(rhs.shape, F32)
    anyspace = pl.BlockSpec(memory_space=pl.ANY)
    peers = sum(sizes[a] - 1 for a in AXES)
    padded = pltpu.VMEM((nf, nx + 2, tall, nz), F32)

    def kernel(*refs):
        main_kernel(sizes, (nf, nx, ny), *refs)

    q1, q2, c = pl.pallas_call(
        kernel,
        out_shape=(field, field, jax.ShapeDtypeStruct((2, 8, 128), F32)),
        in_specs=[anyspace, anyspace],
        out_specs=(anyspace, anyspace, pl.BlockSpec(memory_space=pltpu.VMEM)),
        scratch_shapes=[
            padded, padded,
            pltpu.VMEM((13, nx + 1, tall, nz), F32),
            pltpu.VMEM((len(LO) + len(HI), nx, ny, nz), F32),
            pltpu.VMEM((nx, ny, nz), F32),
            pltpu.VMEM((nx, ny, nz), F32),
            pltpu.VMEM((nf, nx, ny, nz), F32),
            pltpu.VMEM((3, ny // 8, nf + 1, 8, nz), F32),
            pltpu.VMEM((2, nf + 1, 8, nz), F32),
            pltpu.VMEM((2, 2, nf + 1, 8, nz), F32),
            pltpu.VMEM((2, 2, 8, nz), F32),
            pltpu.VMEM((2, 2, 2, 8, nz), F32),
            pltpu.VMEM((len(LO), 8, nz), F32),
            pltpu.VMEM((2, len(LO), 8, nz), F32),
            pltpu.VMEM((nf + 1, 8, nz), F32),
            pltpu.VMEM((2, 8, nz), F32),
            pltpu.VMEM((len(LO), 8, nz), F32),
            pltpu.VMEM((8, 8, 128), F32),
            pltpu.VMEM((8, 128), F32),
            pltpu.VMEM((8, 128), F32),
            pltpu.VMEM((2, 3, 8, 128), F32),
            pltpu.VMEM((2, sizes["gx"], 8, 128), F32),
            pltpu.VMEM((2, sizes["gy"], 8, 128), F32),
            pltpu.VMEM((2, sizes["gz"], 8, 128), F32),
            pltpu.SemaphoreType.DMA((5,)),
            pltpu.SemaphoreType.DMA((40,)),
            pltpu.SemaphoreType.DMA((40,)),
            pltpu.SemaphoreType.DMA((2, peers)),
            pltpu.SemaphoreType.DMA((2, peers)),
        ],
        compiler_params=pltpu.CompilerParams(
            collective_id=0, has_side_effects=True, vmem_limit_bytes=60 * 2**20),
        name="krylov",
    )(rhs, stencil)

    step = 2
    block = pl.BlockSpec((nf, step, ny, nz), lambda i: (0, i, 0, 0))

    def last(*refs):
        final_kernel(ny // 8, step, *refs)

    return pl.pallas_call(
        last,
        grid=(nx // step,),
        out_shape=(field, field),
        in_specs=[pl.BlockSpec(memory_space=pltpu.SMEM), block, block, block],
        out_specs=(block, block),
        scratch_shapes=[pltpu.VMEM((2, 8, 8, 8, 128), F32)],
        compiler_params=pltpu.CompilerParams(dimension_semantics=("arbitrary",), vmem_limit_bytes=60 * 2**20),
        name="combine",
    )(c, rhs, q1, q2)


def solution(mesh):
    sizes = {a: mesh.shape[a] for a in AXES}
    spec = P(None, "gx", "gy", "gz")

    def run(rhs, stencil):
        return shards(sizes, rhs, stencil)

    return jax.shard_map(run, mesh=mesh, in_specs=(spec, spec), out_specs=(spec, spec), check_vma=False)
```

time: 71.7 us -> 57.7 us (0.80)
  Pallas kernels: 70.7 us -> 56.7 us
    pallas_call x1, Pallas kernels: 61.5 us -> 47.5 us  [shards(): pl.pallas_call(kernel, out_shape=(field, field, jax.ShapeDtypeStruct((2,...]
where the time goes in v1:
time: 57.7 us; the launch traced here: 57.4 us
  Pallas kernels  56.7 us (98%)
  between operations  0.64 us (1%)
    pallas_call x1, Pallas kernels, shards(): pl.pallas_call(kernel, out_shape=(field, field, jax.ShapeDtypeStruct((2,...  47.5 us
    pallas_call x1, Pallas kernels, shards(): pl.pallas_call(last, grid=(nx // step,), out_shape=(field, field), in_spe...  9.23 us

profile of v1, /device:TPU:0, one launch (start us, length us, event | category | flops | bytes accessed | tf_op | source)
XLA Modules:
  0.0 57.4 jit_solution(13879722460382707429)
XLA Ops:
  0.6 47.5 %krylov.1 = (f32[8,16,32,128]{3,2,1,0:T(8,128)}, f32[8,16,32,128]{3,2,1,0:T(8,128)}, f32[2,8,128]{2,1,0:T(8,128)}) custom-call(f32[8,16,32,128]{3,2,1,0:T(8,128)} %refs_1_.3, f32[14,16,32,128]{3,2,1,0:T(8,128)} %refs_1_.2), custom_call_target="tpu_custom_call" | custom-call | tf_op jit(solution)/shard_map/krylov/pallas_call | solution.py:614
  48.2 9.2 %combine.1 = (f32[8,16,32,128]{3,2,1,0:T(8,128)}, f32[8,16,32,128]{3,2,1,0:T(8,128)}) custom-call(f32[2,8,128]{2,1,0:T(8,128)} %get-tuple-element.5.refs_0_, f32[8,16,32,128]{3,2,1,0:T(8,128)} %refs_1_.3, f32[8,16,32,128]{3,2,1,0:T(8,128)} %get-tuple-element.6.refs_2_, f32[8,16,32,128]{3,2,1,0:T(8,128)} %get-tuple-element.7.refs_3_), custom_call_target="tpu_custom_call" | custom-call | tf_op jit(solution)/shard_map/combine/pallas_call | solution.py:660

commit v2 on v1

v2 whole, which is shorter than its diff:
```python
import jax
import jax.numpy as jnp
from jax import lax
from jax.experimental import pallas as pl
from jax.experimental.pallas import tpu as pltpu
from jax.sharding import PartitionSpec as P

FORWARD = [
    (a, b, c) for a in (-1, 0, 1) for b in (-1, 0, 1) for c in (-1, 0, 1) if (a, b, c) > (0, 0, 0)
]
AXES = ("gx", "gy", "gz")
LO = [k for k, o in enumerate(FORWARD) if o[2] == 1]
HI = [k for k, o in enumerate(FORWARD) if o[2] == -1]
EX = [k for k, o in enumerate(FORWARD) if o[0] == 1]
F32 = jnp.float32
NS = jax.named_scope


def runs(ks):
    out = []
    for k in ks:
        if out and out[-1][1] == k:
            out[-1][1] = k + 1
        else:
            out.append([k, k + 1])
    return out


def splat(a, k):
    return jnp.broadcast_to(a[:, k : k + 1], (8, 128))


def line(a, k):
    return jnp.broadcast_to(a[k : k + 1, :], (8, 128))


def columns(a):
    return [splat(a, k) for k in range(8)]


def mm(cols, b):
    parts = [cols[k] * line(b, k) for k in range(8)]
    while len(parts) > 1:
        parts = [parts[i] + parts[i + 1] for i in range(0, len(parts), 2)]
    return parts[0]


def solve(cols, b, row):
    cols = list(cols)
    for k in range(8):
        factor = cols[k]
        inverse = 1.0 / line(factor, k)
        pivot = line(b, k) * inverse
        b = jnp.where(row == k, pivot, b - factor * pivot)
        for j in range(k + 1, 8):
            pivot = line(cols[j], k) * inverse
            cols[j] = jnp.where(row == k, pivot, cols[j] - factor * pivot)
    return b


def transposed(a, row, lane):
    out = jnp.zeros_like(a)
    for i in range(8):
        across = jnp.sum(jnp.where(lane == row, a[:, i : i + 1], 0.0), axis=0, keepdims=True)
        out = out + jnp.where(row == i, across, 0.0)
    return out


def main_kernel(sizes, dims, rhs, sten, x1, r1, p1, s1, t_out, p0, q0, w, ws, s0, diag, q2, scr,
                zsend, zrecv, esend, erecv, wzsend, wzrecv, ufull, uedge, uw, red, held, gacc, cur, slots,
                t_alpha, t_beta, t_ib, lsem, xs, xr, ars, arr):
    nf, nx, ny = dims
    yb_n = ny // 8
    tall = ny + 16
    per = 4 * yb_n
    pos = {a: lax.axis_index(a) for a in AXES}
    lane = lax.broadcasted_iota(jnp.int32, (8, 128), 1)
    row = lax.broadcasted_iota(jnp.int32, (8, 128), 0)
    first_lane = lane == 0
    last_lane = lane == 127
    rim = first_lane | last_lane
    even = lax.rem(lane, 2) == 0
    half_lane = lane // 2
    ys = pl.ds(8, ny)
    SHIFTED = LO + HI

    devices = sizes["gx"] * sizes["gy"] * sizes["gz"]
    me = (pos["gx"] * sizes["gy"] + pos["gy"]) * sizes["gz"] + pos["gz"]

    loads = [
        pltpu.make_async_copy(rhs, p0.at[:, pl.ds(1, nx), ys], lsem.at[0]),
        pltpu.make_async_copy(sten.at[pl.ds(1, 13)], w.at[:, pl.ds(1, nx), ys], lsem.at[1]),
        pltpu.make_async_copy(sten.at[0], s0, lsem.at[2]),
    ]
    for copy in loads:
        copy.start()

    moved = {a: [lax.rem(pos[a] + d, sizes[a]) for d in range(sizes[a])] for a in AXES}
    offsets = [(i, j, k) for i in range(sizes["gx"]) for j in range(sizes["gy"]) for k in range(sizes["gz"])][1:]
    offsets.sort(key=lambda d: -sum(min(v, sizes[a] - v) for v, a in zip(d, AXES)))

    def peer(d):
        return {a: moved[a][v] for v, a in zip(d, AXES)}

    barrier = pltpu.get_barrier_semaphore()
    for d in offsets:
        pl.semaphore_signal(barrier, inc=1, device_id=peer(d), device_id_type=pl.DeviceIdType.MESH)

    last = {a: sizes[a] - 1 for a in AXES}

    @pl.when(pos["gx"] == 0)
    def _():
        for buf in (p0, q0):
            buf[:, 0, ys] = jnp.zeros((nf, ny, 128), F32)
        w[:, 0, ys] = jnp.zeros((13, ny, 128), F32)

    @pl.when(pos["gx"] == last["gx"])
    def _():
        for buf in (p0, q0):
            buf[:, nx + 1, ys] = jnp.zeros((nf, ny, 128), F32)

    def clear_y(y):
        def body(x, carry):
            for buf in (p0, q0):
                buf[:, x, y : y + 8] = jnp.zeros((nf, 8, 128), F32)
            return carry

        lax.fori_loop(0, nx + 2, body, 0)

        def body_w(x, carry):
            w[:, x, y : y + 8] = jnp.zeros((13, 8, 128), F32)
            return carry

        lax.fori_loop(0, nx + 1, body_w, 0)

    @pl.when(pos["gy"] == 0)
    def _():
        clear_y(0)

    @pl.when(pos["gy"] == last["gy"])
    def _():
        clear_y(ny + 8)

    for side, place in ((0, 0), (1, last["gz"])):
        @pl.when(pos["gz"] == place)
        def _():
            for e in range(2):
                for part in range(2):
                    zrecv[e, part, side] = jnp.zeros((nf + 1, 8, 128), F32)
                erecv[e, side] = jnp.zeros((2, 8, 128), F32)
            wzrecv[side] = jnp.zeros((len(LO), 8, 128), F32)

    zsend[...] = jnp.zeros(zsend.shape, F32)
    esend[...] = jnp.zeros(esend.shape, F32)
    wzsend[...] = jnp.zeros(wzsend.shape, F32)

    pl.semaphore_wait(barrier, devices - 1)

    count = [0]

    def shift(axis, up, src, dst):
        n = sizes[axis]
        i = pos[axis]
        slot = count[0]
        count[0] += 1
        copy = pltpu.make_async_remote_copy(
            src_ref=src, dst_ref=dst, send_sem=xs.at[slot], recv_sem=xr.at[slot],
            device_id={axis: lax.rem(i + (1 if up else n - 1), n)},
            device_id_type=pl.DeviceIdType.MESH)
        sends = i < n - 1 if up else i > 0
        gets = i > 0 if up else i < n - 1

        @pl.when(sends)
        def _():
            copy.start()

        def finish():
            @pl.when(sends)
            def _():
                copy.wait_send()

            @pl.when(gets)
            def _():
                copy.wait_recv()

        return finish

    def finish_all(items):
        for f in items:
            f()

    def y_faces(buf, start, length):
        xs_ = pl.ds(start, length)
        return [
            shift("gy", True, buf.at[:, xs_, pl.ds(ny, 8)], buf.at[:, xs_, pl.ds(0, 8)]),
            shift("gy", False, buf.at[:, xs_, pl.ds(8, 8)], buf.at[:, xs_, pl.ds(ny + 8, 8)]),
        ]

    def w_faces(start, length, edge):
        xs_ = pl.ds(start, length)
        out = []
        for b, up, src, dst in ((1, True, ny, 0), (-1, False, 8, ny + 8)):
            for lo, hi in runs([k for k, o in enumerate(FORWARD) if o[1] == b and (o[0] or not edge)]):
                ks = pl.ds(lo, hi - lo)
                out.append(shift("gy", up, w.at[ks, xs_, pl.ds(src, 8)], w.at[ks, xs_, pl.ds(dst, 8)]))
        return out

    def x_faces(buf):
        return [
            shift("gx", True, buf.at[:, nx, ys], buf.at[:, 0, ys]),
            shift("gx", False, buf.at[:, 1, ys], buf.at[:, nx + 1, ys]),
        ]

    def z_both(send, recv):
        return [
            shift("gz", True, send, recv.at[0]),
            shift("gz", False, send, recv.at[1]),
        ]

    def gram_body(accs, ub, vb):
        return [accs[i] + ub[i : i + 1] * vb[i:] for i in range(nf)]

    def gram_start():
        return tuple(jnp.zeros((nf - i, 8, 128), F32) for i in range(nf))

    def place(g, i, j):
        return 36 * g + 8 * i - i * (i - 1) // 2 + j - i

    def gram_end(g, accs):
        red[...] = jnp.zeros(red.shape, F32)
        for i in range(nf):
            red[i, i:nf, :] = jnp.sum(accs[i], axis=1)
        out = jnp.zeros((8, 128), F32)
        for i in range(nf):
            t = jnp.sum(red[i], axis=1, keepdims=True)
            out = out + jnp.where(lane == place(g, i, row), t, 0.0)
        return out

    def own(buf):
        return lambda x, yb: buf[:, x + 1, 8 + yb * 8 : 16 + yb * 8]

    def gram_plane(accs, u, v, x):
        for yb in range(yb_n):
            accs = gram_body(accs, u(x, yb), v(x, yb))
        return tuple(accs)

    def gram(g, u, v):
        return gram_end(g, lax.fori_loop(0, nx, lambda x, accs: gram_plane(accs, u, v, x), gram_start()))

    def several(n, f):
        def body(t, carry):
            for k in range(n):
                f(t * n + k, 0)
            return carry

        lax.fori_loop(0, nx // n, body, 0)

    def pack_w(x, carry):
        for yb in range(yb_n):
            j = x * yb_n + yb
            here = half_lane == j
            y = 8 + yb * 8
            for n, k in enumerate(LO):
                both = w[k, x + 1, y : y + 8]
                if n < len(HI):
                    both = jnp.where(first_lane, w[HI[n], x + 1, y : y + 8], both)
                pltpu.store(wzsend.at[n], pltpu.roll(both, 2 * j + 1, 1), mask=here)
        return carry

    def shift_w(x, carry):
        for yb in range(yb_n):
            y = 8 + yb * 8
            for n, k in enumerate(SHIFTED):
                ws[n, x, yb * 8 : yb * 8 + 8] = pltpu.roll(w[k, x + 1, y : y + 8], 1 if k in LO else 127, 1)
        return carry

    def insert_w(x, carry):
        for yb in range(yb_n):
            j = x * yb_n + yb
            for n in range(len(LO)):
                edge = pltpu.roll(uw[n], 127 - 2 * j, 1)
                pltpu.store(ws.at[n, x, yb * 8 : yb * 8 + 8], edge, mask=first_lane)
                if n < len(HI):
                    pltpu.store(ws.at[len(LO) + n, x, yb * 8 : yb * 8 + 8], edge, mask=last_lane)
        return carry

    def crossing(from_low, from_high):
        return jnp.where(even, pltpu.roll(from_high, 127, 1), pltpu.roll(from_low, 1, 1))

    def sums(buf, e, x):
        for yb in range(yb_n):
            y = 8 + yb * 8
            accs = {}
            back = {}
            for a in (-1, 0, 1):
                for b in (-1, 0, 1):
                    v = buf[:, x + 1 + a, y + b : y + b + 8]
                    for c in (-1, 0, 1):
                        o = (a, b, c)
                        if o == (0, 0, 0):
                            continue
                        if o > (0, 0, 0):
                            k = FORWARD.index(o)
                            if c == 0:
                                coef = w[k, x + 1, y : y + 8]
                            else:
                                coef = ws[SHIFTED.index(k), x, yb * 8 : yb * 8 + 8]
                        else:
                            k = FORWARD.index((-a, -b, -c))
                            coef = w[k, x + 1 + a, y + b : y + b + 8]
                            if e == 0:
                                back[c] = coef if c not in back else back[c] + coef
                        term = coef[None] * v
                        accs[c] = term if c not in accs else accs[c] + term
            if e == 0:
                total = s0[x, yb * 8 : yb * 8 + 8] + back[0]
                for k in range(13):
                    total = total + w[k, x + 1, y : y + 8]
                back[0] = total
            for c in (-1, 0, 1):
                scr[c + 1, yb, 0:nf] = accs[c]
                if e == 0:
                    scr[c + 1, yb, nf] = back[c]

    def settle(buf, e, x, put, chunk, where=0):
        for yb in range(yb_n):
            y = 8 + yb * 8
            j = x * yb_n + yb
            edge = where * yb_n + yb
            here = half_lane == j
            if e == 0:
                up, down = scr[2, yb, nf], scr[0, yb, nf]
                total = scr[1, yb, nf] + pltpu.roll(up, 127, 1) + pltpu.roll(down, 1, 1)
                diag[x, yb * 8 : yb * 8 + 8] = total
                both = jnp.where(first_lane, up, down)
                if chunk < 2:
                    pltpu.store(zsend.at[e, chunk, nf], pltpu.roll(both, 2 * j + 1, 1), mask=here)
                else:
                    pltpu.store(esend.at[e, 1], pltpu.roll(both, 2 * edge + 1, 1), mask=half_lane == edge)
            else:
                total = diag[x, yb * 8 : yb * 8 + 8]
            for f in range(nf):
                up, down = scr[2, yb, f], scr[0, yb, f]
                total_f = scr[1, yb, f] + pltpu.roll(up, 127, 1) + pltpu.roll(down, 1, 1)
                put(f, x, yb, total * buf[f, x + 1, y : y + 8] - total_f)
                both = jnp.where(first_lane, up, down)
                if chunk < 2:
                    pltpu.store(zsend.at[e, chunk, f], pltpu.roll(both, 2 * j + 1, 1), mask=here)
                else:
                    m = f * (per // 2) + edge
                    pltpu.store(esend.at[e, 0], pltpu.roll(both, (2 * m + 1) % 128, 1), mask=half_lane == m)

    def gather(e, chunk):
        send, recv = (zsend.at[e, chunk], zrecv.at[e, chunk]) if chunk < 2 else (esend.at[e], erecv.at[e])
        for n in range((nf if chunk < 2 else 1) + 1 - e):
            mine = send[n]
            crossed[chunk][n] = crossing(recv[0, n] - mine, recv[1, n] - mine)

    crossed = [ufull.at[0], ufull.at[1], uedge]

    def mend(buf, e, x, get, put, chunk, where=0):
        for yb in range(yb_n):
            y = 8 + yb * 8
            j = x * yb_n + yb
            edge = where * yb_n + yb
            if e == 0:
                if chunk < 2:
                    extra = pltpu.roll(ufull[chunk, nf], 127 - 2 * j, 1)
                else:
                    extra = pltpu.roll(uedge[1], 127 - 2 * edge, 1)
                extra = jnp.where(rim, extra, 0.0)
                diag[x, yb * 8 : yb * 8 + 8] += extra
            for f in range(nf):
                if chunk < 2:
                    side = pltpu.roll(ufull[chunk, f], 127 - 2 * j, 1)
                else:
                    side = pltpu.roll(uedge[0], 127 - 2 * (f * (per // 2) + edge), 1)
                value = get(f, x, yb) - jnp.where(rim, side, 0.0)
                if e == 0:
                    value = value + extra * buf[f, x + 1, y : y + 8]
                put(f, x, yb, value)

    def copy_row(r, n, dst):
        return pltpu.make_async_remote_copy(
            src_ref=cur.at[r], dst_ref=slots.at[r, dst], send_sem=ars.at[r, n], recv_sem=arr.at[r, n],
            device_id=peer(offsets[n]), device_id_type=pl.DeviceIdType.MESH)

    def sum_start(r, value):
        value = jnp.sum(value, axis=0, keepdims=True)
        cur[r] = value
        slots[r, me] = value
        for n in range(devices - 1):
            copy_row(r, n, me).start()

    def sum_end(r):
        for n, d in enumerate(offsets):
            source = [moved[a][(sizes[a] - v) % sizes[a]] for v, a in zip(d, AXES)]
            copy_row(r, n, me).wait_send()
            copy_row(r, n, (source[0] * sizes["gy"] + source[1]) * sizes["gz"] + source[2]).wait_recv()
        parts = [slots[r, q] for q in range(devices)]
        while len(parts) > 1:
            parts = [a + b for a, b in zip(parts[::2], parts[1::2])] + parts[len(parts) // 2 * 2 :]
        return jnp.broadcast_to(parts[0], (8, 128))

    def extract(total, g):
        cols = []
        for k in range(8):
            where = place(g, jnp.minimum(row, k), jnp.maximum(row, k))
            cols.append(jnp.broadcast_to(jnp.sum(jnp.where(lane == where, total, 0.0), axis=1, keepdims=True), (8, 128)))
        return cols

    def matrix(cols):
        out = jnp.zeros((8, 128), F32)
        for k in range(8):
            out = jnp.where(lane == k, cols[k], out)
        return out

    def fill(tab, cols):
        for j in range(8):
            for i in range(8):
                tab[i, j] = line(cols[j], i)

    k0, k1 = EX[0], EX[-1] + 1

    def put_q1(f, x, yb, v):
        q0[f, x + 1, 8 + yb * 8 : 16 + yb * 8] = v

    def get_q1(f, x, yb):
        return q0[f, x + 1, 8 + yb * 8 : 16 + yb * 8]

    def put_q2(f, x, yb, v):
        q2[f, x, yb * 8 : yb * 8 + 8] = v

    def get_q2(f, x, yb):
        return q2[f, x, yb * 8 : yb * 8 + 8]

    turn = nx - 4

    def planes(buf, e, put, lo, hi, chunk):
        def body(x, carry):
            settle(buf, e, x - 1, put, chunk)
            sums(buf, e, x)
            return carry

        lax.fori_loop(lo, hi, body, 0)

    def operate(buf, e, put, across):
        def z_send(chunk):
            part = pl.ds(0, nf + 1 - e)
            return z_both(zsend.at[e, chunk, part], zrecv.at[e, chunk, :, part])

        with NS(f"op{e}_st1"):
            sums(buf, e, 1)
            planes(buf, e, put, 2, turn, 0)
            sent = [z_send(0)]
        with NS(f"op{e}_xwait"):
            finish_all(across)
            ends = y_faces(buf, 0, 1) + y_faces(buf, nx + 1, 1)
            if e == 0:
                ends += w_faces(0, 1, True)
        with NS(f"op{e}_st2"):
            planes(buf, e, put, turn, nx - 1, 1)
        with NS(f"op{e}_ywait"):
            finish_all(ends)
        with NS(f"op{e}_st3"):
            settle(buf, e, nx - 2, put, 1)
            sums(buf, e, 0)
            sent.append(z_send(1))
            settle(buf, e, 0, put, 2, 0)
            sums(buf, e, nx - 1)
            settle(buf, e, nx - 1, put, 2, 1)
            sent.append(z_both(esend.at[e, pl.ds(0, 2 - e)], erecv.at[e, :, pl.ds(0, 2 - e)]))
        return sent

    with NS("a_load"):
        loads[0].wait()
        sides = y_faces(p0, 1, nx)
        phase = x_faces(p0)
        loads[1].wait()
        sides += w_faces(1, nx, False)
        phase.append(shift("gx", True, w.at[pl.ds(k0, k1 - k0), nx, ys], w.at[pl.ds(k0, k1 - k0), 0, ys]))
    with NS("a_packw"):
        several(8, pack_w)
        zw = z_both(wzsend, wzrecv)
    with NS("a_gram0"):
        gacc[...] = gram(0, own(p0), own(p0))
    with NS("a_shiftw"):
        several(4, shift_w)
    with NS("a_zwait"):
        finish_all(zw)
    with NS("a_insw"):
        for n in range(len(LO)):
            uw[n] = crossing(wzrecv[0, n], wzrecv[1, n])
        several(8, insert_w)
    with NS("a_ywait"):
        loads[2].wait()
        finish_all(sides)
    sent = operate(p0, 0, put_q1, phase)

    def mend_gram(buf, e, get, put, u, v, accs, lo, hi, chunk):
        mend(buf, e, lo, get, put, chunk)

        def body(x, accs):
            accs = gram_plane(accs, u, v, x)
            mend(buf, e, x + 1, get, put, chunk)
            return accs

        return gram_plane(lax.fori_loop(lo, hi - 1, body, accs), u, v, hi - 1)

    cut = turn - 1
    with NS("b_zwait1"):
        finish_all(sent[0])
        gather(0, 0)
    with NS("b_mend1"):
        accs = mend_gram(p0, 0, get_q1, put_q1, own(p0), own(q0), gram_start(), 1, cut, 0)
        sides = y_faces(q0, 2, cut - 1)
    with NS("b_zwait2"):
        finish_all(sent[1])
        gather(0, 1)
    with NS("b_mend2"):
        accs = mend_gram(p0, 0, get_q1, put_q1, own(p0), own(q0), accs, cut, nx - 1, 1)
    with NS("b_gram2a"):
        squares = lax.fori_loop(1, cut, lambda x, accs: gram_plane(accs, own(q0), own(q0), x), gram_start())
        for i in range(nf):
            held[i, i:nf] = squares[i]
    with NS("b_zwait3"):
        finish_all(sent[2])
        gather(0, 2)
    with NS("b_mend3"):
        mend(p0, 0, 0, get_q1, put_q1, 2, 0)
        mend(p0, 0, nx - 1, get_q1, put_q1, 2, 1)
        phase = x_faces(q0)
        sides += y_faces(q0, 1, 1) + y_faces(q0, cut + 1, nx - cut)
    with NS("b_gram1"):
        accs = gram_plane(accs, own(p0), own(q0), 0)
        accs = gram_plane(accs, own(p0), own(q0), nx - 1)
        gacc[...] += gram_end(1, accs)
    with NS("b_gram2"):
        squares = tuple(held[i, i:nf] for i in range(nf))
        squares = gram_plane(squares, own(q0), own(q0), 0)
        squares = lax.fori_loop(cut, nx, lambda x, accs: gram_plane(accs, own(q0), own(q0), x), squares)
        sum_start(0, gacc[...] + gram_end(2, squares))
    with NS("b_ywait"):
        finish_all(sides)

    sent = operate(q0, 1, put_q2, phase)

    def get_v2(x, yb):
        return q2[:, x, yb * 8 : yb * 8 + 8]

    with NS("c_sum1"):
        total = sum_end(0)
    with NS("c_alg1"):
        rrc, pqc, ssc = [extract(total, g) for g in range(3)]
        rr, pq = matrix(rrc), matrix(pqc)
        alpha = solve(pqc, rr, row)
        alpha_c = columns(alpha)
        fill(t_alpha, alpha_c)
        alpha_tc = columns(transposed(alpha, row, lane))
        ssa = mm(ssc, alpha)
        new = rr - mm(alpha_tc, pq) - mm(pqc, alpha) + mm(alpha_tc, ssa)
        beta = solve(rrc, new, row)
        fill(t_beta, columns(beta))
        ib = beta + jnp.where(lane == row, 1.0, 0.0)
        ib_tc = columns(transposed(ib, row, lane))
        fill(t_ib, columns(ib))
        left = mm(ib_tc, mm(pqc, ib) - ssa) - mm(alpha_tc, mm(ssc, ib))

    def early(x, carry):
        for yb in range(yb_n):
            y = slice(yb * 8, yb * 8 + 8)
            u, v = own(p0)(x, yb), own(q0)(x, yb)
            step, rest = t_alpha[0] * u[0][None], u
            for i in range(nf):
                if i:
                    step = step + t_alpha[i] * u[i][None]
                rest = rest - t_alpha[i] * v[i][None]
            x1[:, x, y] = step
            r1[:, x, y] = rest
        return carry

    def late(x, carry):
        for yb in range(yb_n):
            y = slice(yb * 8, yb * 8 + 8)
            u, v, z = own(p0)(x, yb), own(q0)(x, yb), get_v2(x, yb)
            step, image = r1[:, x, y], jnp.zeros((nf, 8, 128), F32)
            for i in range(nf):
                step = step + t_beta[i] * u[i][None]
                image = image + (t_ib[i] * v[i][None] - t_alpha[i] * z[i][None])
            p1[:, x, y] = step
            s1[:, x, y] = image
        return carry

    with NS("c_early"):
        lax.fori_loop(0, nx, early, 0)
    with NS("c_zwait"):
        for n in range(3):
            finish_all(sent[n])
            gather(1, n)
    with NS("c_mend"):
        accs = mend_gram(q0, 1, get_q2, put_q2, own(q0), get_v2, gram_start(), 1, cut, 0)
        accs = mend_gram(q0, 1, get_q2, put_q2, own(q0), get_v2, accs, cut, nx - 1, 1)
        mend(q0, 1, 0, get_q2, put_q2, 2, 0)
        mend(q0, 1, nx - 1, get_q2, put_q2, 2, 1)
        accs = gram_plane(accs, own(q0), get_v2, 0)
        accs = gram_plane(accs, own(q0), get_v2, nx - 1)
        sum_start(1, gram_end(0, accs))
    with NS("c_late"):
        lax.fori_loop(0, nx, late, 0)
    with NS("c_sum2"):
        total = sum_end(1)
    with NS("c_alg2"):
        curve = left + mm(alpha_tc, mm(extract(total, 0), alpha))
        fill(t_out, columns(solve(columns(curve), new, row)))


def final_kernel(dims, step, t, x1, r1, p1, s1, sol, res, sol_buf, res_buf, sem):
    nf, nx, ny = dims

    def saves(n):
        part = pl.ds(n * step, step)
        return [pltpu.make_async_copy(sol_buf.at[:, part], sol.at[:, part], sem.at[0, n]),
                pltpu.make_async_copy(res_buf.at[:, part], res.at[:, part], sem.at[1, n])]

    def body(n, carry):
        for k in range(step):
            x = n * step + k
            for yb in range(ny // 8):
                y = slice(yb * 8, yb * 8 + 8)
                u, v = p1[:, x, y], s1[:, x, y]
                s, e = x1[:, x, y], r1[:, x, y]
                for i in range(nf):
                    s = s + t[i] * u[i][None]
                    e = e - t[i] * v[i][None]
                sol_buf[:, x, y] = s
                res_buf[:, x, y] = e
        for copy in saves(n):
            copy.start()
        return carry

    lax.fori_loop(0, nx // step, body, 0)

    def end(n, carry):
        for copy in saves(n):
            copy.wait()
        return carry

    lax.fori_loop(0, nx // step, end, 0)


def shards(sizes, rhs, stencil):
    nf, nx, ny, nz = rhs.shape
    tall = ny + 16
    field = jax.ShapeDtypeStruct(rhs.shape, F32)
    kept = pltpu.VMEM(rhs.shape, F32)
    table = pltpu.VMEM((8, 8, 8, nz), F32)
    anyspace = pl.BlockSpec(memory_space=pl.ANY)
    local = pl.BlockSpec(memory_space=pltpu.VMEM)
    devices = sizes["gx"] * sizes["gy"] * sizes["gz"]
    padded = pltpu.VMEM((nf, nx + 2, tall, nz), F32)

    def kernel(*refs):
        main_kernel(sizes, (nf, nx, ny), *refs)

    x1, r1, p1, s1, t = pl.pallas_call(
        kernel,
        out_shape=(kept, kept, kept, kept, table),
        in_specs=[pl.BlockSpec(memory_space=pltpu.HBM)] * 2,
        out_specs=(local,) * 5,
        scratch_shapes=[
            padded, padded,
            pltpu.VMEM((13, nx + 1, tall, nz), F32),
            pltpu.VMEM((len(LO) + len(HI), nx, ny, nz), F32),
            pltpu.VMEM((nx, ny, nz), F32),
            pltpu.VMEM((nx, ny, nz), F32),
            pltpu.VMEM((nf, nx, ny, nz), F32),
            pltpu.VMEM((3, ny // 8, nf + 1, 8, nz), F32),
            pltpu.VMEM((2, 2, nf + 1, 8, nz), F32),
            pltpu.VMEM((2, 2, 2, nf + 1, 8, nz), F32),
            pltpu.VMEM((2, 2, 8, nz), F32),
            pltpu.VMEM((2, 2, 2, 8, nz), F32),
            pltpu.VMEM((len(LO), 8, nz), F32),
            pltpu.VMEM((2, len(LO), 8, nz), F32),
            pltpu.VMEM((2, nf + 1, 8, nz), F32),
            pltpu.VMEM((2, 8, nz), F32),
            pltpu.VMEM((len(LO), 8, nz), F32),
            pltpu.VMEM((8, 8, 128), F32),
            pltpu.VMEM((8, 8, 8, 128), F32),
            pltpu.VMEM((8, 128), F32),
            pltpu.VMEM((2, 1, 128), F32),
            pltpu.VMEM((2, devices, 1, 128), F32),
            table, table, table,
            pltpu.SemaphoreType.DMA((3,)),
            pltpu.SemaphoreType.DMA((64,)),
            pltpu.SemaphoreType.DMA((64,)),
            pltpu.SemaphoreType.DMA((2, devices - 1)),
            pltpu.SemaphoreType.DMA((2, devices - 1)),
        ],
        compiler_params=pltpu.CompilerParams(
            collective_id=0, has_side_effects=True, vmem_limit_bytes=40 * 2**20),
        name="krylov",
    )(*[pltpu.with_memory_space_constraint(v, pltpu.HBM) for v in (rhs, stencil)])

    step = 2

    def last(*refs):
        final_kernel((nf, nx, ny), step, *refs)

    return pl.pallas_call(
        last,
        out_shape=(field, field),
        in_specs=[local] * 5,
        out_specs=(pl.BlockSpec(memory_space=pltpu.HBM),) * 2,
        scratch_shapes=[
            pltpu.VMEM(rhs.shape, F32), pltpu.VMEM(rhs.shape, F32),
            pltpu.SemaphoreType.DMA((2, nx // step)),
        ],
        compiler_params=pltpu.CompilerParams(vmem_limit_bytes=40 * 2**20),
        name="combine",
    )(t, x1, r1, p1, s1)


def solution(mesh):
    sizes = {a: mesh.shape[a] for a in AXES}
    spec = P(None, "gx", "gy", "gz")

    def run(rhs, stencil):
        return shards(sizes, rhs, stencil)

    return jax.shard_map(run, mesh=mesh, in_specs=(spec, spec), out_specs=(spec, spec), check_vma=False)
```

time: 57.7 us -> 48 us (0.83)
  Pallas kernels: 56.7 us -> 47.2 us
    pallas_call x2, Pallas kernels: 56.7 us -> 47.2 us  [the longest x1 43.9 us: shards(): pl.pallas_call(kernel, out_shape=(kept, kept, kept, kept, table), in_spec...]
where the time goes in v2:
time: 48 us; the launch traced here: 47.8 us
  Pallas kernels  47.2 us (98%)
  between operations  0.64 us (1%)
    pallas_call x1, Pallas kernels, shards(): pl.pallas_call(kernel, out_shape=(kept, kept, kept, kept, table), in_spec...  43.9 us
    pallas_call x1, Pallas kernels, shards(): pl.pallas_call(last, out_shape=(field, field), in_specs=[local] * 5, out_...  3.21 us

profile of v2, /device:TPU:0, one launch (start us, length us, event | category | flops | bytes accessed | tf_op | source)
XLA Modules:
  0.0 47.8 jit_solution(5887588936761251216)
XLA Ops:
  0.6 43.9 %krylov.1 = (f32[8,16,32,128]{3,2,1,0:T(8,128)S(1)}, f32[8,16,32,128]{3,2,1,0:T(8,128)S(1)}, f32[8,16,32,128]{3,2,1,0:T(8,128)S(1)}, f32[8,16,32,128]{3,2,1,0:T(8,128)S(1)}, f32[8,8,8,128]{3,2,1,0:T(8,128)S(1)}) custom-call(f32[8,16,32,128]{3,2,1,0:T(8,128)} %refs_0_.1, f32[14,16,32,128]{3,2,1,0:T(8,128)} %refs_1_.1), custom_call_target="tpu_custom_call" | custom-call | tf_op jit(solution)/shard_map/krylov/pallas_call | solution.py:665
  44.6 3.2 %combine.1 = (f32[8,16,32,128]{3,2,1,0:T(8,128)}, f32[8,16,32,128]{3,2,1,0:T(8,128)}) custom-call(f32[8,8,8,128]{3,2,1,0:T(8,128)S(1)} %get-tuple-element.7.refs_0_, f32[8,16,32,128]{3,2,1,0:T(8,128)S(1)} %get-tuple-element.8.refs_1_, f32[8,16,32,128]{3,2,1,0:T(8,128)S(1)} %get-tuple-element.9.refs_2_, f32[8,16,32,128]{3,2,1,0:T(8,128)S(1)} %get-tuple-element.10.refs_3_, ...), custom_call_target="tpu_custom_call" | custom-call | tf_op jit(solution)/shard_map/combine/pallas_call | solution.py:709

commit v3 on v2

--- a/solution.py
+++ b/solution.py
@@ -11,7 +11,6 @@
 AXES = ("gx", "gy", "gz")
 LO = [k for k, o in enumerate(FORWARD) if o[2] == 1]
 HI = [k for k, o in enumerate(FORWARD) if o[2] == -1]
-EX = [k for k, o in enumerate(FORWARD) if o[0] == 1]
 F32 = jnp.float32
 NS = jax.named_scope
 
@@ -67,12 +66,15 @@
 
 
 def main_kernel(sizes, dims, rhs, sten, x1, r1, p1, s1, t_out, p0, q0, w, ws, s0, diag, q2, scr,
-                zsend, zrecv, esend, erecv, wzsend, wzrecv, ufull, uedge, uw, red, held, gacc, cur, slots,
+                xsend, xrecv, xpsend, xprecv, zsend, zrecv, wzsend, wzrecv, ucross, uw, red, held, gacc, cur, slots,
                 t_alpha, t_beta, t_ib, lsem, xs, xr, ars, arr):
     nf, nx, ny = dims
     yb_n = ny // 8
     tall = ny + 16
-    per = 4 * yb_n
+    group = 128 // (8 * yb_n)
+    deep = 4
+    wide = deep * yb_n
+    chunks = nx // deep
     pos = {a: lax.axis_index(a) for a in AXES}
     lane = lax.broadcasted_iota(jnp.int32, (8, 128), 1)
     row = lax.broadcasted_iota(jnp.int32, (8, 128), 0)
@@ -92,8 +94,8 @@
         pltpu.make_async_copy(sten.at[pl.ds(1, 13)], w.at[:, pl.ds(1, nx), ys], lsem.at[1]),
         pltpu.make_async_copy(sten.at[0], s0, lsem.at[2]),
     ]
-    for copy in loads:
-        copy.start()
+    loads[1].start()
+    loads[2].start()
 
     moved = {a: [lax.rem(pos[a] + d, sizes[a]) for d in range(sizes[a])] for a in AXES}
     offsets = [(i, j, k) for i in range(sizes["gx"]) for j in range(sizes["gy"]) for k in range(sizes["gz"])][1:]
@@ -110,9 +112,10 @@
 
     @pl.when(pos["gx"] == 0)
     def _():
-        for buf in (p0, q0):
-            buf[:, 0, ys] = jnp.zeros((nf, ny, 128), F32)
-        w[:, 0, ys] = jnp.zeros((13, ny, 128), F32)
+        xrecv[...] = jnp.zeros(xrecv.shape, F32)
+        xprecv[...] = jnp.zeros(xprecv.shape, F32)
+
+    loads[0].start()
 
     @pl.when(pos["gx"] == last["gx"])
     def _():
@@ -125,13 +128,13 @@
                 buf[:, x, y : y + 8] = jnp.zeros((nf, 8, 128), F32)
             return carry
 
-        lax.fori_loop(0, nx + 2, body, 0)
+        lax.fori_loop(1, nx + 2, body, 0)
 
         def body_w(x, carry):
             w[:, x, y : y + 8] = jnp.zeros((13, 8, 128), F32)
             return carry
 
-        lax.fori_loop(0, nx + 1, body_w, 0)
+        lax.fori_loop(1, nx + 1, body_w, 0)
 
     @pl.when(pos["gy"] == 0)
     def _():
@@ -145,13 +148,12 @@
         @pl.when(pos["gz"] == place)
         def _():
             for e in range(2):
-                for part in range(2):
-                    zrecv[e, part, side] = jnp.zeros((nf + 1, 8, 128), F32)
-                erecv[e, side] = jnp.zeros((2, 8, 128), F32)
+                for n in range(chunks):
+                    zrecv[e, n, side] = jnp.zeros(zrecv.shape[3:], F32)
             wzrecv[side] = jnp.zeros((len(LO), 8, 128), F32)
 
     zsend[...] = jnp.zeros(zsend.shape, F32)
-    esend[...] = jnp.zeros(esend.shape, F32)
+    xpsend[...] = jnp.zeros(xpsend.shape, F32)
     wzsend[...] = jnp.zeros(wzsend.shape, F32)
 
     pl.semaphore_wait(barrier, devices - 1)
@@ -196,20 +198,21 @@
             shift("gy", False, buf.at[:, xs_, pl.ds(8, 8)], buf.at[:, xs_, pl.ds(ny + 8, 8)]),
         ]
 
-    def w_faces(start, length, edge):
+    def w_faces(start, length):
         xs_ = pl.ds(start, length)
         out = []
         for b, up, src, dst in ((1, True, ny, 0), (-1, False, 8, ny + 8)):
-            for lo, hi in runs([k for k, o in enumerate(FORWARD) if o[1] == b and (o[0] or not edge)]):
+            for lo, hi in runs([k for k, o in enumerate(FORWARD) if o[1] == b]):
                 ks = pl.ds(lo, hi - lo)
                 out.append(shift("gy", up, w.at[ks, xs_, pl.ds(src, 8)], w.at[ks, xs_, pl.ds(dst, 8)]))
         return out
 
-    def x_faces(buf):
-        return [
-            shift("gx", True, buf.at[:, nx, ys], buf.at[:, 0, ys]),
-            shift("gx", False, buf.at[:, 1, ys], buf.at[:, nx + 1, ys]),
-        ]
+    def x_down(buf):
+        return [shift("gx", False, buf.at[:, 1, ys], buf.at[:, nx + 1, ys])]
+
+    def x_up(e):
+        part = pl.ds(0, nf + 1 - e)
+        return [shift("gx", True, xsend.at[e, part], xrecv.at[e, part]), shift("gx", True, xpsend.at[e, pl.ds(0, packs(e))], xprecv.at[e, pl.ds(0, packs(e))])]
 
     def z_both(send, recv):
         return [
@@ -287,12 +290,43 @@
     def crossing(from_low, from_high):
         return jnp.where(even, pltpu.roll(from_high, 127, 1), pltpu.roll(from_low, 1, 1))
 
-    def sums(buf, e, x):
+    def pack_z(out, f, both, m):
+        m = f % group * wide + m
+        pltpu.store(out.at[f // group], pltpu.roll(both, lax.rem(2 * m + 1, 128), 1), mask=half_lane == m)
+
+    def upward(buf, e):
         for yb in range(yb_n):
             y = 8 + yb * 8
             accs = {}
             back = {}
-            for a in (-1, 0, 1):
+            for b in (-1, 0, 1):
+                v = buf[:, nx, y + b : y + b + 8]
+                for c in (-1, 0, 1):
+                    coef = w[FORWARD.index((1, -b, -c)), nx, y + b : y + b + 8]
+                    term = coef[None] * v
+                    accs[c] = term if c not in accs else accs[c] + term
+                    back[c] = coef if c not in back else back[c] + coef
+            xsend[e, 0:nf, yb * 8 : yb * 8 + 8] = (
+                accs[0] + pltpu.roll(accs[1], 127, 2) + pltpu.roll(accs[-1], 1, 2))
+            both = jnp.where(first_lane[None], accs[1], accs[-1])
+            for f in range(nf):
+                pack_z(xpsend.at[e], f, both[f], (deep - 1) * yb_n + yb)
+            if e == 0:
+                xsend[e, nf, yb * 8 : yb * 8 + 8] = (
+                    back[0] + pltpu.roll(back[1], 127, 1) + pltpu.roll(back[-1], 1, 1))
+                both = jnp.where(first_lane, back[1], back[-1])
+                pack_z(xpsend.at[e], nf, both, (deep - 1) * yb_n + yb)
+
+    def sums(buf, e, x, lowest=False):
+        for yb in range(yb_n):
+            y = 8 + yb * 8
+            accs = {}
+            back = {}
+            if lowest:
+                accs[0] = xrecv[e, 0:nf, yb * 8 : yb * 8 + 8]
+                if e == 0:
+                    back[0] = xrecv[e, nf, yb * 8 : yb * 8 + 8]
+            for a in (0, 1) if lowest else (-1, 0, 1):
                 for b in (-1, 0, 1):
                     v = buf[:, x + 1 + a, y + b : y + b + 8]
                     for c in (-1, 0, 1):
@@ -322,60 +356,46 @@
                 if e == 0:
                     scr[c + 1, yb, nf] = back[c]
 
-    def settle(buf, e, x, put, chunk, where=0):
+    def settle(buf, e, x, put, chunk, where):
         for yb in range(yb_n):
             y = 8 + yb * 8
-            j = x * yb_n + yb
-            edge = where * yb_n + yb
-            here = half_lane == j
+            m = where * yb_n + yb
             if e == 0:
                 up, down = scr[2, yb, nf], scr[0, yb, nf]
                 total = scr[1, yb, nf] + pltpu.roll(up, 127, 1) + pltpu.roll(down, 1, 1)
                 diag[x, yb * 8 : yb * 8 + 8] = total
-                both = jnp.where(first_lane, up, down)
-                if chunk < 2:
-                    pltpu.store(zsend.at[e, chunk, nf], pltpu.roll(both, 2 * j + 1, 1), mask=here)
-                else:
-                    pltpu.store(esend.at[e, 1], pltpu.roll(both, 2 * edge + 1, 1), mask=half_lane == edge)
+                pack_z(zsend.at[e, chunk], nf, jnp.where(first_lane, up, down), m)
             else:
                 total = diag[x, yb * 8 : yb * 8 + 8]
             for f in range(nf):
                 up, down = scr[2, yb, f], scr[0, yb, f]
                 total_f = scr[1, yb, f] + pltpu.roll(up, 127, 1) + pltpu.roll(down, 1, 1)
                 put(f, x, yb, total * buf[f, x + 1, y : y + 8] - total_f)
-                both = jnp.where(first_lane, up, down)
-                if chunk < 2:
-                    pltpu.store(zsend.at[e, chunk, f], pltpu.roll(both, 2 * j + 1, 1), mask=here)
-                else:
-                    m = f * (per // 2) + edge
-                    pltpu.store(esend.at[e, 0], pltpu.roll(both, (2 * m + 1) % 128, 1), mask=half_lane == m)
+                pack_z(zsend.at[e, chunk], f, jnp.where(first_lane, up, down), m)
 
     def gather(e, chunk):
-        send, recv = (zsend.at[e, chunk], zrecv.at[e, chunk]) if chunk < 2 else (esend.at[e], erecv.at[e])
-        for n in range((nf if chunk < 2 else 1) + 1 - e):
-            mine = send[n]
-            crossed[chunk][n] = crossing(recv[0, n] - mine, recv[1, n] - mine)
-
-    crossed = [ufull.at[0], ufull.at[1], uedge]
-
-    def mend(buf, e, x, get, put, chunk, where=0):
+        for n in range(packs(e)):
+            mine = zsend[e, chunk, n]
+            ucross[chunk, n] = crossing(zrecv[e, chunk, 0, n] - mine, zrecv[e, chunk, 1, n] - mine)
+
+    def packs(e):
+        return (nf - e) // group + 1
+
+    def mend(buf, e, x, get, put, chunk, where):
         for yb in range(yb_n):
             y = 8 + yb * 8
-            j = x * yb_n + yb
-            edge = where * yb_n + yb
+            m = where * yb_n + yb
+
+            def edge(f):
+                place = f % group * wide + m
+                side = pltpu.roll(ucross[chunk, f // group], lax.rem(255 - 2 * place, 128), 1)
+                return jnp.where(rim, side, 0.0)
+
             if e == 0:
-                if chunk < 2:
-                    extra = pltpu.roll(ufull[chunk, nf], 127 - 2 * j, 1)
-                else:
-                    extra = pltpu.roll(uedge[1], 127 - 2 * edge, 1)
-                extra = jnp.where(rim, extra, 0.0)
+                extra = edge(nf)
                 diag[x, yb * 8 : yb * 8 + 8] += extra
             for f in range(nf):
-                if chunk < 2:
-                    side = pltpu.roll(ufull[chunk, f], 127 - 2 * j, 1)
-                else:
-                    side = pltpu.roll(uedge[0], 127 - 2 * (f * (per // 2) + edge), 1)
-                value = get(f, x, yb) - jnp.where(rim, side, 0.0)
+                value = get(f, x, yb) - edge(f)
                 if e == 0:
                     value = value + extra * buf[f, x + 1, y : y + 8]
                 put(f, x, yb, value)
@@ -420,8 +440,6 @@
             for i in range(8):
                 tab[i, j] = line(cols[j], i)
 
-    k0, k1 = EX[0], EX[-1] + 1
-
     def put_q1(f, x, yb, v):
         q0[f, x + 1, 8 + yb * 8 : 16 + yb * 8] = v
 
@@ -434,56 +452,93 @@
     def get_q2(f, x, yb):
         return q2[f, x, yb * 8 : yb * 8 + 8]
 
-    turn = nx - 4
-
-    def planes(buf, e, put, lo, hi, chunk):
-        def body(x, carry):
-            settle(buf, e, x - 1, put, chunk)
+    def z_send(e, chunk):
+        part = pl.ds(0, packs(e))
+        return z_both(zsend.at[e, chunk, part], zrecv.at[e, chunk, :, part])
+
+    def planes(buf, e, put, chunk):
+        def body(t, carry):
+            x = chunk * deep + 2 + t
+            settle(buf, e, x - 1, put, chunk, t)
             sums(buf, e, x)
             return carry
 
-        lax.fori_loop(lo, hi, body, 0)
-
-    def operate(buf, e, put, across):
-        def z_send(chunk):
-            part = pl.ds(0, nf + 1 - e)
-            return z_both(zsend.at[e, chunk, part], zrecv.at[e, chunk, :, part])
-
-        with NS(f"op{e}_st1"):
-            sums(buf, e, 1)
-            planes(buf, e, put, 2, turn, 0)
-            sent = [z_send(0)]
+        lax.fori_loop(0, deep, body, 0)
+        return z_send(e, chunk)
+
+    end = chunks - 1
+
+    def interior(buf, e, put, across=None):
+        sent = []
+        ends = None
+        sums(buf, e, 1)
+        for n in range(end):
+            with NS(f"op{e}_in{n}"):
+                sent.append(planes(buf, e, put, n))
+            if across and n == end - 2:
+                ends = arrive(buf, e, across)
+        with NS(f"op{e}_in{end}"):
+            settle(buf, e, nx - 3, put, end, 0)
+            sums(buf, e, nx - 2)
+            settle(buf, e, nx - 2, put, end, 1)
+        return sent, ends
+
+    def arrive(buf, e, across):
         with NS(f"op{e}_xwait"):
             finish_all(across)
-            ends = y_faces(buf, 0, 1) + y_faces(buf, nx + 1, 1)
-            if e == 0:
-                ends += w_faces(0, 1, True)
-        with NS(f"op{e}_st2"):
-            planes(buf, e, put, turn, nx - 1, 1)
+            return y_faces(buf, nx + 1, 1)
+
+    def outer(buf, e, put, ends, across):
         with NS(f"op{e}_ywait"):
             finish_all(ends)
         with NS(f"op{e}_st3"):
-            settle(buf, e, nx - 2, put, 1)
-            sums(buf, e, 0)
-            sent.append(z_send(1))
-            settle(buf, e, 0, put, 2, 0)
             sums(buf, e, nx - 1)
-            settle(buf, e, nx - 1, put, 2, 1)
-            sent.append(z_both(esend.at[e, pl.ds(0, 2 - e)], erecv.at[e, :, pl.ds(0, 2 - e)]))
-        return sent
-
-    with NS("a_load"):
-        loads[0].wait()
-        sides = y_faces(p0, 1, nx)
-        phase = x_faces(p0)
+            settle(buf, e, nx - 1, put, end, 2)
+        with NS(f"op{e}_upwait"):
+            finish_all(across)
+        with NS(f"op{e}_st4"):
+            sums(buf, e, 0, True)
+            settle(buf, e, 0, put, end, 3)
+            for n in range(packs(e)):
+                zsend[e, end, n] += xprecv[e, n]
+            return z_send(e, end)
+
+    def mend_gram(buf, e, get, put, u, v, accs, chunk):
+        lo = chunk * deep + 1
+        mend(buf, e, lo, get, put, chunk, 0)
+
+        def body(t, accs):
+            accs = gram_plane(accs, u, v, lo + t)
+            mend(buf, e, lo + t + 1, get, put, chunk, t + 1)
+            return accs
+
+        return gram_plane(lax.fori_loop(0, deep - 1, body, accs), u, v, lo + deep - 1)
+
+    def mend_end(buf, e, get, put, between=None):
+        for where, x in ((2, nx - 1), (3, 0), (0, nx - 3), (1, nx - 2)):
+            mend(buf, e, x, get, put, end, where)
+            if between and where == 2:
+                between()
+
+    rest = (nx - 1, 0, nx - 3, nx - 2)
+
+    with NS("a_loadw"):
         loads[1].wait()
-        sides += w_faces(1, nx, False)
-        phase.append(shift("gx", True, w.at[pl.ds(k0, k1 - k0), nx, ys], w.at[pl.ds(k0, k1 - k0), 0, ys]))
+        rims = w_faces(nx, 1)
     with NS("a_packw"):
         several(8, pack_w)
         zw = z_both(wzsend, wzrecv)
+    with NS("a_loadp"):
+        loads[0].wait()
+        rims += y_faces(p0, nx, 1)
+        down = x_down(p0)
+        sides = y_faces(p0, 1, nx - 1) + w_faces(1, nx - 1)
     with NS("a_gram0"):
         gacc[...] = gram(0, own(p0), own(p0))
+    with NS("a_up"):
+        finish_all(rims)
+        upward(p0, 0)
+        up = x_up(0)
     with NS("a_shiftw"):
         several(4, shift_w)
     with NS("a_zwait"):
@@ -495,55 +550,46 @@
     with NS("a_ywait"):
         loads[2].wait()
         finish_all(sides)
-    sent = operate(p0, 0, put_q1, phase)
-
-    def mend_gram(buf, e, get, put, u, v, accs, lo, hi, chunk):
-        mend(buf, e, lo, get, put, chunk)
-
-        def body(x, accs):
-            accs = gram_plane(accs, u, v, x)
-            mend(buf, e, x + 1, get, put, chunk)
-            return accs
-
-        return gram_plane(lax.fori_loop(lo, hi - 1, body, accs), u, v, hi - 1)
-
-    cut = turn - 1
-    with NS("b_zwait1"):
-        finish_all(sent[0])
-        gather(0, 0)
-    with NS("b_mend1"):
-        accs = mend_gram(p0, 0, get_q1, put_q1, own(p0), own(q0), gram_start(), 1, cut, 0)
-        sides = y_faces(q0, 2, cut - 1)
-    with NS("b_zwait2"):
-        finish_all(sent[1])
-        gather(0, 1)
-    with NS("b_mend2"):
-        accs = mend_gram(p0, 0, get_q1, put_q1, own(p0), own(q0), accs, cut, nx - 1, 1)
+    sent, ends = interior(p0, 0, put_q1, down)
+    sent.append(outer(p0, 0, put_q1, ends, up))
+
+    accs = gram_start()
+    sides = []
+    for n in range(end):
+        with NS(f"b_zwait{n}"):
+            finish_all(sent[n])
+            gather(0, n)
+        with NS(f"b_mend{n}"):
+            accs = mend_gram(p0, 0, get_q1, put_q1, own(p0), own(q0), accs, n)
+            sides += y_faces(q0, n * deep + 2, deep)
+    with NS(f"b_zwait{end}"):
+        finish_all(sent[end])
+        gather(0, end)
+    rims = []
+    with NS(f"b_mend{end}"):
+        mend_end(p0, 0, get_q1, put_q1, lambda: rims.extend(y_faces(q0, nx, 1)))
+        sides += y_faces(q0, 1, 1) + y_faces(q0, nx - 2, 2)
+    with NS("b_gram1"):
+        for x in rest:
+            accs = gram_plane(accs, own(p0), own(q0), x)
+        gacc[...] += gram_end(1, accs)
     with NS("b_gram2a"):
-        squares = lax.fori_loop(1, cut, lambda x, accs: gram_plane(accs, own(q0), own(q0), x), gram_start())
+        down = x_down(q0)
+        squares = lax.fori_loop(1, nx, lambda x, accs: gram_plane(accs, own(q0), own(q0), x), gram_start())
         for i in range(nf):
             held[i, i:nf] = squares[i]
-    with NS("b_zwait3"):
-        finish_all(sent[2])
-        gather(0, 2)
-    with NS("b_mend3"):
-        mend(p0, 0, 0, get_q1, put_q1, 2, 0)
-        mend(p0, 0, nx - 1, get_q1, put_q1, 2, 1)
-        phase = x_faces(q0)
-        sides += y_faces(q0, 1, 1) + y_faces(q0, cut + 1, nx - cut)
-    with NS("b_gram1"):
-        accs = gram_plane(accs, own(p0), own(q0), 0)
-        accs = gram_plane(accs, own(p0), own(q0), nx - 1)
-        gacc[...] += gram_end(1, accs)
+    with NS("b_up"):
+        finish_all(rims)
+        upward(q0, 1)
+        up = x_up(1)
     with NS("b_gram2"):
         squares = tuple(held[i, i:nf] for i in range(nf))
         squares = gram_plane(squares, own(q0), own(q0), 0)
-        squares = lax.fori_loop(cut, nx, lambda x, accs: gram_plane(accs, own(q0), own(q0), x), squares)
         sum_start(0, gacc[...] + gram_end(2, squares))
     with NS("b_ywait"):
         finish_all(sides)
 
-    sent = operate(q0, 1, put_q2, phase)
+    sent, ends = interior(q0, 1, put_q2)
 
     def get_v2(x, yb):
         return q2[:, x, yb * 8 : yb * 8 + 8]
@@ -591,20 +637,28 @@
             s1[:, x, y] = image
         return carry
 
+    split = nx // 4
+    ends = arrive(q0, 1, down)
     with NS("c_early"):
-        lax.fori_loop(0, nx, early, 0)
-    with NS("c_zwait"):
-        for n in range(3):
+        lax.fori_loop(0, split, early, 0)
+    sent.append(outer(q0, 1, put_q2, ends, up))
+    accs = gram_start()
+    for n in range(end):
+        with NS(f"c_zwait{n}"):
             finish_all(sent[n])
             gather(1, n)
-    with NS("c_mend"):
-        accs = mend_gram(q0, 1, get_q2, put_q2, own(q0), get_v2, gram_start(), 1, cut, 0)
-        accs = mend_gram(q0, 1, get_q2, put_q2, own(q0), get_v2, accs, cut, nx - 1, 1)
-        mend(q0, 1, 0, get_q2, put_q2, 2, 0)
-        mend(q0, 1, nx - 1, get_q2, put_q2, 2, 1)
-        accs = gram_plane(accs, own(q0), get_v2, 0)
-        accs = gram_plane(accs, own(q0), get_v2, nx - 1)
+        with NS(f"c_mend{n}"):
+            accs = mend_gram(q0, 1, get_q2, put_q2, own(q0), get_v2, accs, n)
+    with NS(f"c_zwait{end}"):
+        finish_all(sent[end])
+        gather(1, end)
+    with NS(f"c_mend{end}"):
+        mend_end(q0, 1, get_q2, put_q2)
+        for x in rest:
+            accs = gram_plane(accs, own(q0), get_v2, x)
         sum_start(1, gram_end(0, accs))
+    with NS("c_early2"):
+        lax.fori_loop(split, nx, early, 0)
     with NS("c_late"):
         lax.fori_loop(0, nx, late, 0)
     with NS("c_sum2"):
@@ -657,6 +711,7 @@
     anyspace = pl.BlockSpec(memory_space=pl.ANY)
     local = pl.BlockSpec(memory_space=pltpu.VMEM)
     devices = sizes["gx"] * sizes["gy"] * sizes["gz"]
+    chunks, packs = nx // 4, nf // (16 // (ny // 8)) + 1
     padded = pltpu.VMEM((nf, nx + 2, tall, nz), F32)
 
     def kernel(*refs):
@@ -675,14 +730,15 @@
             pltpu.VMEM((nx, ny, nz), F32),
             pltpu.VMEM((nf, nx, ny, nz), F32),
             pltpu.VMEM((3, ny // 8, nf + 1, 8, nz), F32),
-            pltpu.VMEM((2, 2, nf + 1, 8, nz), F32),
-            pltpu.VMEM((2, 2, 2, nf + 1, 8, nz), F32),
-            pltpu.VMEM((2, 2, 8, nz), F32),
-            pltpu.VMEM((2, 2, 2, 8, nz), F32),
+            pltpu.VMEM((2, nf + 1, ny, nz), F32),
+            pltpu.VMEM((2, nf + 1, ny, nz), F32),
+            pltpu.VMEM((2, packs, 8, nz), F32),
+            pltpu.VMEM((2, packs, 8, nz), F32),
+            pltpu.VMEM((2, chunks, packs, 8, nz), F32),
+            pltpu.VMEM((2, chunks, 2, packs, 8, nz), F32),
             pltpu.VMEM((len(LO), 8, nz), F32),
             pltpu.VMEM((2, len(LO), 8, nz), F32),
-            pltpu.VMEM((2, nf + 1, 8, nz), F32),
-            pltpu.VMEM((2, 8, nz), F32),
+            pltpu.VMEM((chunks, packs, 8, nz), F32),
             pltpu.VMEM((len(LO), 8, nz), F32),
             pltpu.VMEM((8, 8, 128), F32),
             pltpu.VMEM((8, 8, 8, 128), F32),

time: 48 us -> 43.7 us (0.910)
  Pallas kernels: 47.2 us -> 42.9 us
    pallas_call x1, Pallas kernels: 43.9 us -> 39.7 us  [shards(): pl.pallas_call(kernel, out_shape=(kept, kept, kept, kept, table), in_spec...]
where the time goes in v3:
time: 43.7 us; the launch traced here: 43.6 us
  Pallas kernels  42.9 us (98%)
  between operations  0.64 us (1%)
    pallas_call x1, Pallas kernels, shards(): pl.pallas_call(kernel, out_shape=(kept, kept, kept, kept, table), in_spec...  39.7 us
    pallas_call x1, Pallas kernels, shards(): pl.pallas_call(last, out_shape=(field, field), in_specs=[local] * 5, out_...  3.21 us

profile of v3, /device:TPU:0, one launch (start us, length us, event | category | flops | bytes accessed | tf_op | source)
XLA Modules:
  0.0 43.6 jit_solution(6712292767898244344)
XLA Ops:
  0.6 39.7 %krylov.1 = (f32[8,16,32,128]{3,2,1,0:T(8,128)S(1)}, f32[8,16,32,128]{3,2,1,0:T(8,128)S(1)}, f32[8,16,32,128]{3,2,1,0:T(8,128)S(1)}, f32[8,16,32,128]{3,2,1,0:T(8,128)S(1)}, f32[8,8,8,128]{3,2,1,0:T(8,128)S(1)}) custom-call(f32[8,16,32,128]{3,2,1,0:T(8,128)} %refs_0_.1, f32[14,16,32,128]{3,2,1,0:T(8,128)} %refs_1_.1), custom_call_target="tpu_custom_call" | custom-call | tf_op jit(solution)/shard_map/krylov/pallas_call | solution.py:720
  40.4 3.2 %combine.1 = (f32[8,16,32,128]{3,2,1,0:T(8,128)}, f32[8,16,32,128]{3,2,1,0:T(8,128)}) custom-call(f32[8,8,8,128]{3,2,1,0:T(8,128)S(1)} %get-tuple-element.7.refs_0_, f32[8,16,32,128]{3,2,1,0:T(8,128)S(1)} %get-tuple-element.8.refs_1_, f32[8,16,32,128]{3,2,1,0:T(8,128)S(1)} %get-tuple-element.9.refs_2_, f32[8,16,32,128]{3,2,1,0:T(8,128)S(1)} %get-tuple-element.10.refs_3_, ...), custom_call_target="tpu_custom_call" | custom-call | tf_op jit(solution)/shard_map/combine/pallas_call | solution.py:765

commit v4 on v3

--- a/solution.py
+++ b/solution.py
@@ -9,6 +9,8 @@
     (a, b, c) for a in (-1, 0, 1) for b in (-1, 0, 1) for c in (-1, 0, 1) if (a, b, c) > (0, 0, 0)
 ]
 AXES = ("gx", "gy", "gz")
+RECEIVES = 37
+SENDS = 20
 LO = [k for k, o in enumerate(FORWARD) if o[2] == 1]
 HI = [k for k, o in enumerate(FORWARD) if o[2] == -1]
 F32 = jnp.float32
@@ -66,7 +68,7 @@
 
 
 def main_kernel(sizes, dims, rhs, sten, x1, r1, p1, s1, t_out, p0, q0, w, ws, s0, diag, q2, scr,
-                xsend, xrecv, xpsend, xprecv, zsend, zrecv, wzsend, wzrecv, ucross, uw, red, held, gacc, cur, slots,
+                xsend, xrecv, zsend, zrecv, wzsend, wzrecv, ucross, uw, red, held, gacc, cur, slots,
                 t_alpha, t_beta, t_ib, lsem, xs, xr, ars, arr):
     nf, nx, ny = dims
     yb_n = ny // 8
@@ -75,6 +77,10 @@
     deep = 4
     wide = deep * yb_n
     chunks = nx // deep
+
+    def packs(e):
+        return (nf - e) // group + 1
+
     pos = {a: lax.axis_index(a) for a in AXES}
     lane = lax.broadcasted_iota(jnp.int32, (8, 128), 1)
     row = lax.broadcasted_iota(jnp.int32, (8, 128), 0)
@@ -113,7 +119,6 @@
     @pl.when(pos["gx"] == 0)
     def _():
         xrecv[...] = jnp.zeros(xrecv.shape, F32)
-        xprecv[...] = jnp.zeros(xprecv.shape, F32)
 
     loads[0].start()
 
@@ -153,20 +158,22 @@
             wzrecv[side] = jnp.zeros((len(LO), 8, 128), F32)
 
     zsend[...] = jnp.zeros(zsend.shape, F32)
-    xpsend[...] = jnp.zeros(xpsend.shape, F32)
+    for e in range(2):
+        for n in range(packs(e)):
+            xsend[e, n] = jnp.zeros((8, 128), F32)
     wzsend[...] = jnp.zeros(wzsend.shape, F32)
 
     pl.semaphore_wait(barrier, devices - 1)
 
-    count = [0]
+    arrivals = iter(range(RECEIVES))
+    free = list(range(SENDS))
 
     def shift(axis, up, src, dst):
         n = sizes[axis]
         i = pos[axis]
-        slot = count[0]
-        count[0] += 1
+        slot = free.pop(0)
         copy = pltpu.make_async_remote_copy(
-            src_ref=src, dst_ref=dst, send_sem=xs.at[slot], recv_sem=xr.at[slot],
+            src_ref=src, dst_ref=dst, send_sem=xs.at[slot], recv_sem=xr.at[next(arrivals)],
             device_id={axis: lax.rem(i + (1 if up else n - 1), n)},
             device_id_type=pl.DeviceIdType.MESH)
         sends = i < n - 1 if up else i > 0
@@ -184,6 +191,8 @@
             @pl.when(gets)
             def _():
                 copy.wait_recv()
+
+            free.append(slot)
 
         return finish
 
@@ -210,9 +219,12 @@
     def x_down(buf):
         return [shift("gx", False, buf.at[:, 1, ys], buf.at[:, nx + 1, ys])]
 
+    def x_tile(f, yb):
+        return packs(0) + f * yb_n + yb
+
     def x_up(e):
-        part = pl.ds(0, nf + 1 - e)
-        return [shift("gx", True, xsend.at[e, part], xrecv.at[e, part]), shift("gx", True, xpsend.at[e, pl.ds(0, packs(e))], xprecv.at[e, pl.ds(0, packs(e))])]
+        part = pl.ds(0, x_tile(nf - e, yb_n))
+        return [shift("gx", True, xsend.at[e, part], xrecv.at[e, part])]
 
     def z_both(send, recv):
         return [
@@ -306,16 +318,16 @@
                     term = coef[None] * v
                     accs[c] = term if c not in accs else accs[c] + term
                     back[c] = coef if c not in back else back[c] + coef
-            xsend[e, 0:nf, yb * 8 : yb * 8 + 8] = (
-                accs[0] + pltpu.roll(accs[1], 127, 2) + pltpu.roll(accs[-1], 1, 2))
+            whole = accs[0] + pltpu.roll(accs[1], 127, 2) + pltpu.roll(accs[-1], 1, 2)
             both = jnp.where(first_lane[None], accs[1], accs[-1])
             for f in range(nf):
-                pack_z(xpsend.at[e], f, both[f], (deep - 1) * yb_n + yb)
+                xsend[e, x_tile(f, yb)] = whole[f]
+                pack_z(xsend.at[e], f, both[f], (deep - 1) * yb_n + yb)
             if e == 0:
-                xsend[e, nf, yb * 8 : yb * 8 + 8] = (
+                xsend[e, x_tile(nf, yb)] = (
                     back[0] + pltpu.roll(back[1], 127, 1) + pltpu.roll(back[-1], 1, 1))
                 both = jnp.where(first_lane, back[1], back[-1])
-                pack_z(xpsend.at[e], nf, both, (deep - 1) * yb_n + yb)
+                pack_z(xsend.at[e], nf, both, (deep - 1) * yb_n + yb)
 
     def sums(buf, e, x, lowest=False):
         for yb in range(yb_n):
@@ -323,9 +335,9 @@
             accs = {}
             back = {}
             if lowest:
-                accs[0] = xrecv[e, 0:nf, yb * 8 : yb * 8 + 8]
+                accs[0] = jnp.stack([xrecv[e, x_tile(f, yb)] for f in range(nf)])
                 if e == 0:
-                    back[0] = xrecv[e, nf, yb * 8 : yb * 8 + 8]
+                    back[0] = xrecv[e, x_tile(nf, yb)]
             for a in (0, 1) if lowest else (-1, 0, 1):
                 for b in (-1, 0, 1):
                     v = buf[:, x + 1 + a, y + b : y + b + 8]
@@ -378,9 +390,6 @@
             mine = zsend[e, chunk, n]
             ucross[chunk, n] = crossing(zrecv[e, chunk, 0, n] - mine, zrecv[e, chunk, 1, n] - mine)
 
-    def packs(e):
-        return (nf - e) // group + 1
-
     def mend(buf, e, x, get, put, chunk, where):
         for yb in range(yb_n):
             y = 8 + yb * 8
@@ -402,7 +411,7 @@
 
     def copy_row(r, n, dst):
         return pltpu.make_async_remote_copy(
-            src_ref=cur.at[r], dst_ref=slots.at[r, dst], send_sem=ars.at[r, n], recv_sem=arr.at[r, n],
+            src_ref=cur.at[r], dst_ref=slots.at[r, dst], send_sem=ars.at[r], recv_sem=arr.at[r],
             device_id=peer(offsets[n]), device_id_type=pl.DeviceIdType.MESH)
 
     def sum_start(r, value):
@@ -413,10 +422,12 @@
             copy_row(r, n, me).start()
 
     def sum_end(r):
-        for n, d in enumerate(offsets):
-            source = [moved[a][(sizes[a] - v) % sizes[a]] for v, a in zip(d, AXES)]
-            copy_row(r, n, me).wait_send()
-            copy_row(r, n, (source[0] * sizes["gy"] + source[1]) * sizes["gz"] + source[2]).wait_recv()
+        every = slots.at[r, pl.ds(0, devices - 1)]
+        copies = pltpu.make_async_remote_copy(
+            src_ref=every, dst_ref=every, send_sem=ars.at[r], recv_sem=arr.at[r],
+            device_id=peer(offsets[0]), device_id_type=pl.DeviceIdType.MESH)
+        copies.wait_send()
+        copies.wait_recv()
         parts = [slots[r, q] for q in range(devices)]
         while len(parts) > 1:
             parts = [a + b for a, b in zip(parts[::2], parts[1::2])] + parts[len(parts) // 2 * 2 :]
@@ -500,7 +511,7 @@
             sums(buf, e, 0, True)
             settle(buf, e, 0, put, end, 3)
             for n in range(packs(e)):
-                zsend[e, end, n] += xprecv[e, n]
+                zsend[e, end, n] += xrecv[e, n]
             return z_send(e, end)
 
     def mend_gram(buf, e, get, put, u, v, accs, chunk):
@@ -524,7 +535,7 @@
 
     with NS("a_loadw"):
         loads[1].wait()
-        rims = w_faces(nx, 1)
+        rims = w_faces(1, nx)
     with NS("a_packw"):
         several(8, pack_w)
         zw = z_both(wzsend, wzrecv)
@@ -532,15 +543,15 @@
         loads[0].wait()
         rims += y_faces(p0, nx, 1)
         down = x_down(p0)
-        sides = y_faces(p0, 1, nx - 1) + w_faces(1, nx - 1)
+        sides = y_faces(p0, 1, nx - 1)
     with NS("a_gram0"):
         gacc[...] = gram(0, own(p0), own(p0))
+    with NS("a_shiftw"):
+        several(4, shift_w)
     with NS("a_up"):
         finish_all(rims)
         upward(p0, 0)
         up = x_up(0)
-    with NS("a_shiftw"):
-        several(4, shift_w)
     with NS("a_zwait"):
         finish_all(zw)
     with NS("a_insw"):
@@ -561,14 +572,13 @@
             gather(0, n)
         with NS(f"b_mend{n}"):
             accs = mend_gram(p0, 0, get_q1, put_q1, own(p0), own(q0), accs, n)
-            sides += y_faces(q0, n * deep + 2, deep)
     with NS(f"b_zwait{end}"):
         finish_all(sent[end])
         gather(0, end)
     rims = []
     with NS(f"b_mend{end}"):
         mend_end(p0, 0, get_q1, put_q1, lambda: rims.extend(y_faces(q0, nx, 1)))
-        sides += y_faces(q0, 1, 1) + y_faces(q0, nx - 2, 2)
+        sides = y_faces(q0, 1, nx - 1)
     with NS("b_gram1"):
         for x in rest:
             accs = gram_plane(accs, own(p0), own(q0), x)
@@ -578,14 +588,14 @@
         squares = lax.fori_loop(1, nx, lambda x, accs: gram_plane(accs, own(q0), own(q0), x), gram_start())
         for i in range(nf):
             held[i, i:nf] = squares[i]
+    with NS("b_gram2"):
+        squares = tuple(held[i, i:nf] for i in range(nf))
+        squares = gram_plane(squares, own(q0), own(q0), 0)
+        sum_start(0, gacc[...] + gram_end(2, squares))
     with NS("b_up"):
         finish_all(rims)
         upward(q0, 1)
         up = x_up(1)
-    with NS("b_gram2"):
-        squares = tuple(held[i, i:nf] for i in range(nf))
-        squares = gram_plane(squares, own(q0), own(q0), 0)
-        sum_start(0, gacc[...] + gram_end(2, squares))
     with NS("b_ywait"):
         finish_all(sides)
 
@@ -673,8 +683,8 @@
 
     def saves(n):
         part = pl.ds(n * step, step)
-        return [pltpu.make_async_copy(sol_buf.at[:, part], sol.at[:, part], sem.at[0, n]),
-                pltpu.make_async_copy(res_buf.at[:, part], res.at[:, part], sem.at[1, n])]
+        return [pltpu.make_async_copy(sol_buf.at[:, part], sol.at[:, part], sem.at[0]),
+                pltpu.make_async_copy(res_buf.at[:, part], res.at[:, part], sem.at[1])]
 
     def body(n, carry):
         for k in range(step):
@@ -694,12 +704,8 @@
 
     lax.fori_loop(0, nx // step, body, 0)
 
-    def end(n, carry):
-        for copy in saves(n):
-            copy.wait()
-        return carry
-
-    lax.fori_loop(0, nx // step, end, 0)
+    pltpu.make_async_copy(sol_buf, sol, sem.at[0]).wait()
+    pltpu.make_async_copy(res_buf, res, sem.at[1]).wait()
 
 
 def shards(sizes, rhs, stencil):
@@ -730,10 +736,8 @@
             pltpu.VMEM((nx, ny, nz), F32),
             pltpu.VMEM((nf, nx, ny, nz), F32),
             pltpu.VMEM((3, ny // 8, nf + 1, 8, nz), F32),
-            pltpu.VMEM((2, nf + 1, ny, nz), F32),
-            pltpu.VMEM((2, nf + 1, ny, nz), F32),
-            pltpu.VMEM((2, packs, 8, nz), F32),
-            pltpu.VMEM((2, packs, 8, nz), F32),
+            pltpu.VMEM((2, packs + (nf + 1) * ny // 8, 8, nz), F32),
+            pltpu.VMEM((2, packs + (nf + 1) * ny // 8, 8, nz), F32),
             pltpu.VMEM((2, chunks, packs, 8, nz), F32),
             pltpu.VMEM((2, chunks, 2, packs, 8, nz), F32),
             pltpu.VMEM((len(LO), 8, nz), F32),
@@ -747,10 +751,10 @@
             pltpu.VMEM((2, devices, 1, 128), F32),
             table, table, table,
             pltpu.SemaphoreType.DMA((3,)),
-            pltpu.SemaphoreType.DMA((64,)),
-            pltpu.SemaphoreType.DMA((64,)),
-            pltpu.SemaphoreType.DMA((2, devices - 1)),
-            pltpu.SemaphoreType.DMA((2, devices - 1)),
+            pltpu.SemaphoreType.DMA((SENDS,)),
+            pltpu.SemaphoreType.DMA((RECEIVES,)),
+            pltpu.SemaphoreType.DMA((2,)),
+            pltpu.SemaphoreType.DMA((2,)),
         ],
         compiler_params=pltpu.CompilerParams(
             collective_id=0, has_side_effects=True, vmem_limit_bytes=40 * 2**20),
@@ -769,7 +773,7 @@
         out_specs=(pl.BlockSpec(memory_space=pltpu.HBM),) * 2,
         scratch_shapes=[
             pltpu.VMEM(rhs.shape, F32), pltpu.VMEM(rhs.shape, F32),
-            pltpu.SemaphoreType.DMA((2, nx // step)),
+            pltpu.SemaphoreType.DMA((2,)),
         ],
         compiler_params=pltpu.CompilerParams(vmem_limit_bytes=40 * 2**20),
         name="combine",

time: 43.7 us -> 41 us (0.938)
  Pallas kernels: 42.9 us -> 40.2 us
    pallas_call x1, Pallas kernels: 39.7 us -> 37.1 us  [shards(): pl.pallas_call(kernel, out_shape=(kept, kept, kept, kept, table), in_spec...]
where the time goes in v4:
time: 41 us; the launch traced here: 40.8 us
  Pallas kernels  40.2 us (98%)
  between operations  0.64 us (2%)
    pallas_call x1, Pallas kernels, shards(): pl.pallas_call(kernel, out_shape=(kept, kept, kept, kept, table), in_spec...  37.1 us
    pallas_call x1, Pallas kernels, shards(): pl.pallas_call(last, out_shape=(field, field), in_specs=[local] * 5, out_...  3.08 us

profile of v4, /device:TPU:0, one launch (start us, length us, event | category | flops | bytes accessed | tf_op | source)
XLA Modules:
  0.0 40.8 jit_solution(1024066637005142020)
XLA Ops:
  0.6 37.1 %krylov.1 = (f32[8,16,32,128]{3,2,1,0:T(8,128)S(1)}, f32[8,16,32,128]{3,2,1,0:T(8,128)S(1)}, f32[8,16,32,128]{3,2,1,0:T(8,128)S(1)}, f32[8,16,32,128]{3,2,1,0:T(8,128)S(1)}, f32[8,8,8,128]{3,2,1,0:T(8,128)S(1)}) custom-call(f32[8,16,32,128]{3,2,1,0:T(8,128)} %refs_0_.1, f32[14,16,32,128]{3,2,1,0:T(8,128)} %refs_1_.1), custom_call_target="tpu_custom_call" | custom-call | tf_op jit(solution)/shard_map/krylov/pallas_call | solution.py:726
  37.7 3.1 %combine.1 = (f32[8,16,32,128]{3,2,1,0:T(8,128)}, f32[8,16,32,128]{3,2,1,0:T(8,128)}) custom-call(f32[8,8,8,128]{3,2,1,0:T(8,128)S(1)} %get-tuple-element.7.refs_0_, f32[8,16,32,128]{3,2,1,0:T(8,128)S(1)} %get-tuple-element.8.refs_1_, f32[8,16,32,128]{3,2,1,0:T(8,128)S(1)} %get-tuple-element.9.refs_2_, f32[8,16,32,128]{3,2,1,0:T(8,128)S(1)} %get-tuple-element.10.refs_3_, ...), custom_call_target="tpu_custom_call" | custom-call | tf_op jit(solution)/shard_map/combine/pallas_call | solution.py:769

commit v5 on v4

--- a/solution.py
+++ b/solution.py
@@ -9,8 +9,8 @@
     (a, b, c) for a in (-1, 0, 1) for b in (-1, 0, 1) for c in (-1, 0, 1) if (a, b, c) > (0, 0, 0)
 ]
 AXES = ("gx", "gy", "gz")
-RECEIVES = 37
-SENDS = 20
+RECEIVES = 40
+SENDS = 16
 LO = [k for k, o in enumerate(FORWARD) if o[2] == 1]
 HI = [k for k, o in enumerate(FORWARD) if o[2] == -1]
 F32 = jnp.float32
@@ -67,9 +67,9 @@
     return out
 
 
-def main_kernel(sizes, dims, rhs, sten, x1, r1, p1, s1, t_out, p0, q0, w, ws, s0, diag, q2, scr,
-                xsend, xrecv, zsend, zrecv, wzsend, wzrecv, ucross, uw, red, held, gacc, cur, slots,
-                t_alpha, t_beta, t_ib, lsem, xs, xr, ars, arr):
+def main_kernel(sizes, dims, rhs, sten, x1, r1, p1, s1, t_out, p0, q0, w, ws, s0, diag, q2, scr, csend, crecv,
+                xsend, xrecv, ysend, yrecv, zsend, zrecv, wzsend, wzrecv, ucross, uw, red, held, gacc, cur, slots,
+                t_alpha, t_beta, t_ib, lsem, xs, xr, ars, arr, ready):
     nf, nx, ny = dims
     yb_n = ny // 8
     tall = ny + 16
@@ -111,8 +111,15 @@
         return {a: moved[a][v] for v, a in zip(d, AXES)}
 
     barrier = pltpu.get_barrier_semaphore()
-    for d in offsets:
-        pl.semaphore_signal(barrier, inc=1, device_id=peer(d), device_id_type=pl.DeviceIdType.MESH)
+    lines = [d for d in offsets if sum(v > 0 for v in d) == 1]
+    across = {(i % sizes["gx"], j % sizes["gy"], 0) for i in (1, -1) for j in (1, -1)}
+    met = lines + sorted(across & set(offsets) - set(lines))
+
+    def tell(sem, d):
+        pl.semaphore_signal(sem, inc=1, device_id=peer(d), device_id_type=pl.DeviceIdType.MESH)
+
+    for d in met:
+        tell(barrier, d)
 
     last = {a: sizes[a] - 1 for a in AXES}
 
@@ -121,6 +128,12 @@
         xrecv[...] = jnp.zeros(xrecv.shape, F32)
 
     loads[0].start()
+
+    for side, place in ((0, 0), (1, last["gy"])):
+        @pl.when((pos["gx"] == last["gx"]) | (pos["gy"] == place))
+        def _():
+            for e in range(2):
+                crecv[e, side] = jnp.zeros((nf, 128), F32)
 
     @pl.when(pos["gx"] == last["gx"])
     def _():
@@ -129,11 +142,10 @@
 
     def clear_y(y):
         def body(x, carry):
-            for buf in (p0, q0):
-                buf[:, x, y : y + 8] = jnp.zeros((nf, 8, 128), F32)
+            p0[:, x, y : y + 8] = jnp.zeros((nf, 8, 128), F32)
             return carry
 
-        lax.fori_loop(1, nx + 2, body, 0)
+        lax.fori_loop(1, nx + 1, body, 0)
 
         def body_w(x, carry):
             w[:, x, y : y + 8] = jnp.zeros((13, 8, 128), F32)
@@ -144,10 +156,12 @@
     @pl.when(pos["gy"] == 0)
     def _():
         clear_y(0)
+        yrecv[0] = jnp.zeros((nx, nf, 128), F32)
 
     @pl.when(pos["gy"] == last["gy"])
     def _():
         clear_y(ny + 8)
+        yrecv[1] = jnp.zeros((nx, nf, 128), F32)
 
     for side, place in ((0, 0), (1, last["gz"])):
         @pl.when(pos["gz"] == place)
@@ -163,7 +177,10 @@
             xsend[e, n] = jnp.zeros((8, 128), F32)
     wzsend[...] = jnp.zeros(wzsend.shape, F32)
 
-    pl.semaphore_wait(barrier, devices - 1)
+    pl.semaphore_wait(barrier, len(met))
+    for d in lines:
+        if d[0]:
+            tell(ready.at[0], d)
 
     arrivals = iter(range(RECEIVES))
     free = list(range(SENDS))
@@ -207,6 +224,26 @@
             shift("gy", False, buf.at[:, xs_, pl.ds(8, 8)], buf.at[:, xs_, pl.ds(ny + 8, 8)]),
         ]
 
+    def y_rows(start, length):
+        part = pl.ds(start, length)
+        return [
+            shift("gy", True, ysend.at[0, part], yrecv.at[0, part]),
+            shift("gy", False, ysend.at[1, part], yrecv.at[1, part]),
+        ]
+
+    def y_unpack(start, length):
+        def body(x, carry):
+            for f in range(nf):
+                q0[f, x + 1, 7:8] = yrecv[0, x, f : f + 1]
+                q0[f, x + 1, ny + 8 : ny + 9] = yrecv[1, x, f : f + 1]
+            return carry
+
+        if length > 3:
+            lax.fori_loop(start, start + length, body, 0)
+        else:
+            for x in range(start, start + length):
+                body(x, 0)
+
     def w_faces(start, length):
         xs_ = pl.ds(start, length)
         out = []
@@ -216,8 +253,44 @@
                 out.append(shift("gy", up, w.at[ks, xs_, pl.ds(src, 8)], w.at[ks, xs_, pl.ds(dst, 8)]))
         return out
 
-    def x_down(buf):
-        return [shift("gx", False, buf.at[:, 1, ys], buf.at[:, nx + 1, ys])]
+    def corner(e, up):
+        side = 0 if up else 1
+        i, j = pos["gx"], pos["gy"]
+        slot = free.pop(0)
+        copy = pltpu.make_async_remote_copy(
+            src_ref=csend.at[e, side], dst_ref=crecv.at[e, side], send_sem=xs.at[slot], recv_sem=xr.at[next(arrivals)],
+            device_id={"gx": moved["gx"][-1], "gy": moved["gy"][1 if up else -1]},
+            device_id_type=pl.DeviceIdType.MESH)
+        sends = (i > 0) & (j < last["gy"] if up else j > 0)
+        gets = (i < last["gx"]) & (j > 0 if up else j < last["gy"])
+
+        @pl.when(sends)
+        def _():
+            copy.start()
+
+        def finish():
+            @pl.when(sends)
+            def _():
+                copy.wait_send()
+
+            @pl.when(gets)
+            def _():
+                copy.wait_recv()
+
+            free.append(slot)
+
+        return finish
+
+    def x_down(buf, e):
+        for f in range(nf):
+            csend[e, 0, f : f + 1] = buf[f, 1, ny + 7 : ny + 8]
+            csend[e, 1, f : f + 1] = buf[f, 1, 8:9]
+        return [shift("gx", False, buf.at[:, 1, ys], buf.at[:, nx + 1, ys]), corner(e, True), corner(e, False)]
+
+    def corners(buf, e):
+        for f in range(nf):
+            buf[f, nx + 1, 7:8] = crecv[e, 0, f : f + 1]
+            buf[f, nx + 1, ny + 8 : ny + 9] = crecv[e, 1, f : f + 1]
 
     def x_tile(f, yb):
         return packs(0) + f * yb_n + yb
@@ -407,6 +480,10 @@
                 value = get(f, x, yb) - edge(f)
                 if e == 0:
                     value = value + extra * buf[f, x + 1, y : y + 8]
+                    if yb == yb_n - 1:
+                        ysend[0, x, f : f + 1] = value[7:8]
+                    if yb == 0:
+                        ysend[1, x, f : f + 1] = value[0:1]
                 put(f, x, yb, value)
 
     def copy_row(r, n, dst):
@@ -479,35 +556,25 @@
 
     end = chunks - 1
 
-    def interior(buf, e, put, across=None):
+    def interior(buf, e, put):
         sent = []
-        ends = None
         sums(buf, e, 1)
         for n in range(end):
             with NS(f"op{e}_in{n}"):
                 sent.append(planes(buf, e, put, n))
-            if across and n == end - 2:
-                ends = arrive(buf, e, across)
         with NS(f"op{e}_in{end}"):
             settle(buf, e, nx - 3, put, end, 0)
             sums(buf, e, nx - 2)
             settle(buf, e, nx - 2, put, end, 1)
-        return sent, ends
-
-    def arrive(buf, e, across):
+        return sent
+
+    def outer(buf, e, put, across):
         with NS(f"op{e}_xwait"):
             finish_all(across)
-            return y_faces(buf, nx + 1, 1)
-
-    def outer(buf, e, put, ends, across):
-        with NS(f"op{e}_ywait"):
-            finish_all(ends)
         with NS(f"op{e}_st3"):
+            corners(buf, e)
             sums(buf, e, nx - 1)
             settle(buf, e, nx - 1, put, end, 2)
-        with NS(f"op{e}_upwait"):
-            finish_all(across)
-        with NS(f"op{e}_st4"):
             sums(buf, e, 0, True)
             settle(buf, e, 0, put, end, 3)
             for n in range(packs(e)):
@@ -515,18 +582,14 @@
             return z_send(e, end)
 
     def mend_gram(buf, e, get, put, u, v, accs, chunk):
-        lo = chunk * deep + 1
-        mend(buf, e, lo, get, put, chunk, 0)
-
-        def body(t, accs):
-            accs = gram_plane(accs, u, v, lo + t)
-            mend(buf, e, lo + t + 1, get, put, chunk, t + 1)
-            return accs
-
-        return gram_plane(lax.fori_loop(0, deep - 1, body, accs), u, v, lo + deep - 1)
+        for t in range(deep):
+            x = chunk * deep + 1 + t
+            mend(buf, e, x, get, put, chunk, t)
+            accs = gram_plane(accs, u, v, x)
+        return accs
 
     def mend_end(buf, e, get, put, between=None):
-        for where, x in ((2, nx - 1), (3, 0), (0, nx - 3), (1, nx - 2)):
+        for where, x in ((0, nx - 3), (1, nx - 2), (2, nx - 1), (3, 0)):
             mend(buf, e, x, get, put, end, where)
             if between and where == 2:
                 between()
@@ -542,7 +605,7 @@
     with NS("a_loadp"):
         loads[0].wait()
         rims += y_faces(p0, nx, 1)
-        down = x_down(p0)
+        down = x_down(p0, 0)
         sides = y_faces(p0, 1, nx - 1)
     with NS("a_gram0"):
         gacc[...] = gram(0, own(p0), own(p0))
@@ -558,48 +621,72 @@
         for n in range(len(LO)):
             uw[n] = crossing(wzrecv[0, n], wzrecv[1, n])
         several(8, insert_w)
+    pl.semaphore_wait(ready.at[0], sizes["gx"] - 1)
+    for d in lines:
+        if d[1]:
+            tell(ready.at[1], d)
     with NS("a_ywait"):
         loads[2].wait()
         finish_all(sides)
-    sent, ends = interior(p0, 0, put_q1, down)
-    sent.append(outer(p0, 0, put_q1, ends, up))
+    sent = interior(p0, 0, put_q1)
+    sent.append(outer(p0, 0, put_q1, down + up))
+
+    def squares(lo, hi, accs):
+        return lax.fori_loop(lo, hi, lambda x, accs: gram_plane(accs, own(q0), own(q0), x), accs)
+
+    def hold(n, accs):
+        for i in range(nf):
+            held[n, i, i:nf] = accs[i]
+
+    def resume(n):
+        return tuple(held[n, i, i:nf] for i in range(nf))
 
     accs = gram_start()
-    sides = []
     for n in range(end):
         with NS(f"b_zwait{n}"):
             finish_all(sent[n])
             gather(0, n)
         with NS(f"b_mend{n}"):
             accs = mend_gram(p0, 0, get_q1, put_q1, own(p0), own(q0), accs, n)
+        if n:
+            with NS(f"b_square{n}"):
+                hold(0, accs)
+                if n == end - 1:
+                    sides = y_rows(1, end * deep)
+                start = 1 if n == 1 else n * deep + 1
+                hold(1, squares(start, (n + 1) * deep + 1, gram_start() if n == 1 else resume(1)))
+                accs = resume(0)
     with NS(f"b_zwait{end}"):
         finish_all(sent[end])
         gather(0, end)
     rims = []
     with NS(f"b_mend{end}"):
-        mend_end(p0, 0, get_q1, put_q1, lambda: rims.extend(y_faces(q0, nx, 1)))
-        sides = y_faces(q0, 1, nx - 1)
+        mend_end(p0, 0, get_q1, put_q1, lambda: rims.extend(y_rows(nx - 3, 3)))
+        sides += y_rows(0, 1)
     with NS("b_gram1"):
         for x in rest:
             accs = gram_plane(accs, own(p0), own(q0), x)
         gacc[...] += gram_end(1, accs)
-    with NS("b_gram2a"):
-        down = x_down(q0)
-        squares = lax.fori_loop(1, nx, lambda x, accs: gram_plane(accs, own(q0), own(q0), x), gram_start())
-        for i in range(nf):
-            held[i, i:nf] = squares[i]
     with NS("b_gram2"):
-        squares = tuple(held[i, i:nf] for i in range(nf))
-        squares = gram_plane(squares, own(q0), own(q0), 0)
-        sum_start(0, gacc[...] + gram_end(2, squares))
+        down = x_down(q0, 1)
+        both = resume(1)
+        for x in rest:
+            both = gram_plane(both, own(q0), own(q0), x)
+        both = gram_end(2, both)
+    pl.semaphore_wait(ready.at[1], sizes["gy"] - 1)
+    with NS("b_sum"):
+        sum_start(0, gacc[...] + both)
     with NS("b_up"):
         finish_all(rims)
+        y_unpack(nx - 3, 3)
         upward(q0, 1)
         up = x_up(1)
     with NS("b_ywait"):
         finish_all(sides)
-
-    sent, ends = interior(q0, 1, put_q2)
+        y_unpack(1, end * deep)
+        y_unpack(0, 1)
+
+    sent = interior(q0, 1, put_q2)
 
     def get_v2(x, yb):
         return q2[:, x, yb * 8 : yb * 8 + 8]
@@ -647,11 +734,10 @@
             s1[:, x, y] = image
         return carry
 
-    split = nx // 4
-    ends = arrive(q0, 1, down)
-    with NS("c_early"):
-        lax.fori_loop(0, split, early, 0)
-    sent.append(outer(q0, 1, put_q2, ends, up))
+    first, second = nx // 8, nx // 2
+    with NS("c_early0"):
+        lax.fori_loop(0, first, early, 0)
+    sent.append(outer(q0, 1, put_q2, down + up))
     accs = gram_start()
     for n in range(end):
         with NS(f"c_zwait{n}"):
@@ -659,6 +745,8 @@
             gather(1, n)
         with NS(f"c_mend{n}"):
             accs = mend_gram(q0, 1, get_q2, put_q2, own(q0), get_v2, accs, n)
+    with NS("c_early1"):
+        lax.fori_loop(first, second, early, 0)
     with NS(f"c_zwait{end}"):
         finish_all(sent[end])
         gather(1, end)
@@ -668,7 +756,7 @@
             accs = gram_plane(accs, own(q0), get_v2, x)
         sum_start(1, gram_end(0, accs))
     with NS("c_early2"):
-        lax.fori_loop(split, nx, early, 0)
+        lax.fori_loop(second, nx, early, 0)
     with NS("c_late"):
         lax.fori_loop(0, nx, late, 0)
     with NS("c_sum2"):
@@ -736,8 +824,12 @@
             pltpu.VMEM((nx, ny, nz), F32),
             pltpu.VMEM((nf, nx, ny, nz), F32),
             pltpu.VMEM((3, ny // 8, nf + 1, 8, nz), F32),
+            pltpu.VMEM((2, 2, nf, nz), F32),
+            pltpu.VMEM((2, 2, nf, nz), F32),
             pltpu.VMEM((2, packs + (nf + 1) * ny // 8, 8, nz), F32),
             pltpu.VMEM((2, packs + (nf + 1) * ny // 8, 8, nz), F32),
+            pltpu.VMEM((2, nx, nf, nz), F32),
+            pltpu.VMEM((2, nx, nf, nz), F32),
             pltpu.VMEM((2, chunks, packs, 8, nz), F32),
             pltpu.VMEM((2, chunks, 2, packs, 8, nz), F32),
             pltpu.VMEM((len(LO), 8, nz), F32),
@@ -745,7 +837,7 @@
             pltpu.VMEM((chunks, packs, 8, nz), F32),
             pltpu.VMEM((len(LO), 8, nz), F32),
             pltpu.VMEM((8, 8, 128), F32),
-            pltpu.VMEM((8, 8, 8, 128), F32),
+            pltpu.VMEM((2, 8, 8, 8, 128), F32),
             pltpu.VMEM((8, 128), F32),
             pltpu.VMEM((2, 1, 128), F32),
             pltpu.VMEM((2, devices, 1, 128), F32),
@@ -755,6 +847,7 @@
             pltpu.SemaphoreType.DMA((RECEIVES,)),
             pltpu.SemaphoreType.DMA((2,)),
             pltpu.SemaphoreType.DMA((2,)),
+            pltpu.SemaphoreType.REGULAR((2,)),
         ],
         compiler_params=pltpu.CompilerParams(
             collective_id=0, has_side_effects=True, vmem_limit_bytes=40 * 2**20),

time: 41 us -> 39.2 us (0.956)
  Pallas kernels: 40.2 us -> 38.4 us
    pallas_call x1, Pallas kernels: 37.1 us -> 35.3 us  [shards(): pl.pallas_call(kernel, out_shape=(kept, kept, kept, kept, table), in_spec...]
where the time goes in v5:
time: 39.2 us; the launch traced here: 39 us
  Pallas kernels  38.4 us (98%)
  between operations  0.64 us (2%)
    pallas_call x1, Pallas kernels, shards(): pl.pallas_call(kernel, out_shape=(kept, kept, kept, kept, table), in_spec...  35.3 us
    pallas_call x1, Pallas kernels, shards(): pl.pallas_call(last, out_shape=(field, field), in_specs=[local] * 5, out_...  3.08 us

profile of v5, /device:TPU:0, one launch (start us, length us, event | category | flops | bytes accessed | tf_op | source)
XLA Modules:
  0.0 39.0 jit_solution(10725995544213129903)
XLA Ops:
  0.6 35.3 %krylov.1 = (f32[8,16,32,128]{3,2,1,0:T(8,128)S(1)}, f32[8,16,32,128]{3,2,1,0:T(8,128)S(1)}, f32[8,16,32,128]{3,2,1,0:T(8,128)S(1)}, f32[8,16,32,128]{3,2,1,0:T(8,128)S(1)}, f32[8,8,8,128]{3,2,1,0:T(8,128)S(1)}) custom-call(f32[8,16,32,128]{3,2,1,0:T(8,128)} %refs_0_.1, f32[14,16,32,128]{3,2,1,0:T(8,128)} %refs_1_.1), custom_call_target="tpu_custom_call" | custom-call | tf_op jit(solution)/shard_map/krylov/pallas_call | solution.py:814
  35.9 3.1 %combine.1 = (f32[8,16,32,128]{3,2,1,0:T(8,128)}, f32[8,16,32,128]{3,2,1,0:T(8,128)}) custom-call(f32[8,8,8,128]{3,2,1,0:T(8,128)S(1)} %get-tuple-element.7.refs_0_, f32[8,16,32,128]{3,2,1,0:T(8,128)S(1)} %get-tuple-element.8.refs_1_, f32[8,16,32,128]{3,2,1,0:T(8,128)S(1)} %get-tuple-element.9.refs_2_, f32[8,16,32,128]{3,2,1,0:T(8,128)S(1)} %get-tuple-element.10.refs_3_, ...), custom_call_target="tpu_custom_call" | custom-call | tf_op jit(solution)/shard_map/combine/pallas_call | solution.py:862

commit v6 on v5

--- a/solution.py
+++ b/solution.py
@@ -67,9 +67,43 @@
     return out
 
 
+def halves(v):
+    v = v.reshape(64, 128)
+    high = v.astype(jnp.bfloat16)
+    low = (v - high.astype(F32)).astype(jnp.bfloat16)
+    return jnp.concatenate([high, low], axis=0)
+
+
+def mixed(coefs, tiles):
+    out = jnp.dot(coefs, jnp.concatenate([halves(v) for v in tiles], axis=1), preferred_element_type=F32)
+    half = out.shape[0] // 2
+    out = out[:half] + out[half:]
+    return [[out[m : m + 64, n * 128 : n * 128 + 128].reshape(8, 8, 128) for n in range(len(tiles))]
+            for m in range(0, half, 64)]
+
+
+def spread(cols, row, lane):
+    slot = lax.rem(lane // 8, 8)
+    high, low = [], []
+    for j in range(8):
+        block = jnp.zeros((8, 128), F32)
+        for i in range(8):
+            block = jnp.where(slot == i, line(cols[j], i), block)
+        block = jnp.where(lax.rem(lane, 8) == row, block, 0.0)
+        near = block.astype(jnp.bfloat16).astype(F32)
+        high.append(near)
+        low.append(jnp.where(lane < 64, block - near, 0.0))
+    return high, low
+
+
+def stacked(parts):
+    rows = [v for high, low in parts for v in high] + [v for high, low in parts for v in low]
+    return jnp.concatenate(rows, axis=0).astype(jnp.bfloat16)
+
+
 def main_kernel(sizes, dims, rhs, sten, x1, r1, p1, s1, t_out, p0, q0, w, ws, s0, diag, q2, scr, csend, crecv,
                 xsend, xrecv, ysend, yrecv, zsend, zrecv, wzsend, wzrecv, ucross, uw, red, held, gacc, cur, slots,
-                t_alpha, t_beta, t_ib, lsem, xs, xr, ars, arr, ready):
+                t_rhs, t_one, t_two, lsem, xs, xr, ars, arr, ready):
     nf, nx, ny = dims
     yb_n = ny // 8
     tall = ny + 16
@@ -522,11 +556,6 @@
         for k in range(8):
             out = jnp.where(lane == k, cols[k], out)
         return out
-
-    def fill(tab, cols):
-        for j in range(8):
-            for i in range(8):
-                tab[i, j] = line(cols[j], i)
 
     def put_q1(f, x, yb, v):
         q0[f, x + 1, 8 + yb * 8 : 16 + yb * 8] = v
@@ -698,45 +727,31 @@
         rr, pq = matrix(rrc), matrix(pqc)
         alpha = solve(pqc, rr, row)
         alpha_c = columns(alpha)
-        fill(t_alpha, alpha_c)
         alpha_tc = columns(transposed(alpha, row, lane))
         ssa = mm(ssc, alpha)
         new = rr - mm(alpha_tc, pq) - mm(pqc, alpha) + mm(alpha_tc, ssa)
         beta = solve(rrc, new, row)
-        fill(t_beta, columns(beta))
         ib = beta + jnp.where(lane == row, 1.0, 0.0)
         ib_tc = columns(transposed(ib, row, lane))
-        fill(t_ib, columns(ib))
+        wide_a, wide_b, wide_i = [spread(c, row, lane) for c in (alpha_c, columns(beta), columns(ib))]
+        t_rhs[...] = stacked([wide_a, wide_b])
+        t_one[...] = stacked([wide_a, wide_i])
+        t_two[...] = stacked([wide_a])
         left = mm(ib_tc, mm(pqc, ib) - ssa) - mm(alpha_tc, mm(ssc, ib))
 
-    def early(x, carry):
+    def late(x):
+        u, v, z = [[g(x, yb) for yb in range(yb_n)] for g in (own(p0), own(q0), get_v2)]
+        step, turn = mixed(t_rhs[...], u)
+        drop, grow = mixed(t_one[...], v)
+        (fall,) = mixed(t_two[...], z)
         for yb in range(yb_n):
             y = slice(yb * 8, yb * 8 + 8)
-            u, v = own(p0)(x, yb), own(q0)(x, yb)
-            step, rest = t_alpha[0] * u[0][None], u
-            for i in range(nf):
-                if i:
-                    step = step + t_alpha[i] * u[i][None]
-                rest = rest - t_alpha[i] * v[i][None]
-            x1[:, x, y] = step
-            r1[:, x, y] = rest
-        return carry
-
-    def late(x, carry):
-        for yb in range(yb_n):
-            y = slice(yb * 8, yb * 8 + 8)
-            u, v, z = own(p0)(x, yb), own(q0)(x, yb), get_v2(x, yb)
-            step, image = r1[:, x, y], jnp.zeros((nf, 8, 128), F32)
-            for i in range(nf):
-                step = step + t_beta[i] * u[i][None]
-                image = image + (t_ib[i] * v[i][None] - t_alpha[i] * z[i][None])
-            p1[:, x, y] = step
-            s1[:, x, y] = image
-        return carry
-
-    first, second = nx // 8, nx // 2
-    with NS("c_early0"):
-        lax.fori_loop(0, first, early, 0)
+            left_over = u[yb] - drop[yb]
+            x1[:, x, y] = step[yb]
+            r1[:, x, y] = left_over
+            p1[:, x, y] = left_over + turn[yb]
+            s1[:, x, y] = grow[yb] - fall[yb]
+
     sent.append(outer(q0, 1, put_q2, down + up))
     accs = gram_start()
     for n in range(end):
@@ -745,8 +760,6 @@
             gather(1, n)
         with NS(f"c_mend{n}"):
             accs = mend_gram(q0, 1, get_q2, put_q2, own(q0), get_v2, accs, n)
-    with NS("c_early1"):
-        lax.fori_loop(first, second, early, 0)
     with NS(f"c_zwait{end}"):
         finish_all(sent[end])
         gather(1, end)
@@ -755,15 +768,13 @@
         for x in rest:
             accs = gram_plane(accs, own(q0), get_v2, x)
         sum_start(1, gram_end(0, accs))
-    with NS("c_early2"):
-        lax.fori_loop(second, nx, early, 0)
     with NS("c_late"):
-        lax.fori_loop(0, nx, late, 0)
+        several(4, lambda x, carry: late(x))
     with NS("c_sum2"):
         total = sum_end(1)
     with NS("c_alg2"):
         curve = left + mm(alpha_tc, mm(extract(total, 0), alpha))
-        fill(t_out, columns(solve(columns(curve), new, row)))
+        t_out[...] = stacked([spread(columns(solve(columns(curve), new, row)), row, lane)])
 
 
 def final_kernel(dims, step, t, x1, r1, p1, s1, sol, res, sol_buf, res_buf, sem):
@@ -774,18 +785,18 @@
         return [pltpu.make_async_copy(sol_buf.at[:, part], sol.at[:, part], sem.at[0]),
                 pltpu.make_async_copy(res_buf.at[:, part], res.at[:, part], sem.at[1])]
 
+    blocks = [slice(yb * 8, yb * 8 + 8) for yb in range(ny // 8)]
+
+    def applied(d, x):
+        return mixed(t[...], [d[:, x, y] for y in blocks])[0]
+
     def body(n, carry):
         for k in range(step):
             x = n * step + k
-            for yb in range(ny // 8):
-                y = slice(yb * 8, yb * 8 + 8)
-                u, v = p1[:, x, y], s1[:, x, y]
-                s, e = x1[:, x, y], r1[:, x, y]
-                for i in range(nf):
-                    s = s + t[i] * u[i][None]
-                    e = e - t[i] * v[i][None]
-                sol_buf[:, x, y] = s
-                res_buf[:, x, y] = e
+            for y, v in zip(blocks, applied(p1, x)):
+                sol_buf[:, x, y] = x1[:, x, y] + v
+            for y, v in zip(blocks, applied(s1, x)):
+                res_buf[:, x, y] = r1[:, x, y] - v
         for copy in saves(n):
             copy.start()
         return carry
@@ -801,7 +812,6 @@
     tall = ny + 16
     field = jax.ShapeDtypeStruct(rhs.shape, F32)
     kept = pltpu.VMEM(rhs.shape, F32)
-    table = pltpu.VMEM((8, 8, 8, nz), F32)
     anyspace = pl.BlockSpec(memory_space=pl.ANY)
     local = pl.BlockSpec(memory_space=pltpu.VMEM)
     devices = sizes["gx"] * sizes["gy"] * sizes["gz"]
@@ -813,7 +823,7 @@
 
     x1, r1, p1, s1, t = pl.pallas_call(
         kernel,
-        out_shape=(kept, kept, kept, kept, table),
+        out_shape=(kept, kept, kept, kept, pltpu.VMEM((128, 128), jnp.bfloat16)),
         in_specs=[pl.BlockSpec(memory_space=pltpu.HBM)] * 2,
         out_specs=(local,) * 5,
         scratch_shapes=[
@@ -841,7 +851,9 @@
             pltpu.VMEM((8, 128), F32),
             pltpu.VMEM((2, 1, 128), F32),
             pltpu.VMEM((2, devices, 1, 128), F32),
-            table, table, table,
+            pltpu.VMEM((256, 128), jnp.bfloat16),
+            pltpu.VMEM((256, 128), jnp.bfloat16),
+            pltpu.VMEM((128, 128), jnp.bfloat16),
             pltpu.SemaphoreType.DMA((3,)),
             pltpu.SemaphoreType.DMA((SENDS,)),
             pltpu.SemaphoreType.DMA((RECEIVES,)),
@@ -854,7 +866,7 @@
         name="krylov",
     )(*[pltpu.with_memory_space_constraint(v, pltpu.HBM) for v in (rhs, stencil)])
 
-    step = 2
+    step = 4
 
     def last(*refs):
         final_kernel((nf, nx, ny), step, *refs)

time: 39.2 us -> 38.8 us (0.990)
  Pallas kernels: 38.4 us -> 38 us
    pallas_call x1, Pallas kernels: 3.08 us -> 2.66 us  [shards(): pl.pallas_call(last, out_shape=(field, field), in_specs=[local] * 5, out_...]
where the time goes in v6:
time: 38.8 us; the launch traced here: 38.6 us
  Pallas kernels  38 us (98%)
  between operations  0.64 us (2%)
    pallas_call x1, Pallas kernels, shards(): pl.pallas_call(kernel, out_shape=(kept, kept, kept, kept, pltpu.VMEM((128...  35.3 us
    pallas_call x1, Pallas kernels, shards(): pl.pallas_call(last, out_shape=(field, field), in_specs=[local] * 5, out_...  2.66 us

profile of v6, /device:TPU:0, one launch (start us, length us, event | category | flops | bytes accessed | tf_op | source)
XLA Modules:
  0.0 38.6 jit_solution(3039211101204565855)
XLA Ops:
  0.6 35.3 %krylov.1 = (f32[8,16,32,128]{3,2,1,0:T(8,128)S(1)}, f32[8,16,32,128]{3,2,1,0:T(8,128)S(1)}, f32[8,16,32,128]{3,2,1,0:T(8,128)S(1)}, f32[8,16,32,128]{3,2,1,0:T(8,128)S(1)}, bf16[128,128]{1,0:T(8,128)(2,1)S(1)}) custom-call(f32[8,16,32,128]{3,2,1,0:T(8,128)} %refs_0_.1, f32[14,16,32,128]{3,2,1,0:T(8,128)} %refs_1_.1), custom_call_target="tpu_custom_call" | custom-call | tf_op jit(solution)/shard_map/krylov/pallas_call | solution.py:824
  35.9 2.7 %combine.1 = (f32[8,16,32,128]{3,2,1,0:T(8,128)}, f32[8,16,32,128]{3,2,1,0:T(8,128)}) custom-call(bf16[128,128]{1,0:T(8,128)(2,1)S(1)} %get-tuple-element.7.refs_0_, f32[8,16,32,128]{3,2,1,0:T(8,128)S(1)} %get-tuple-element.8.refs_1_, f32[8,16,32,128]{3,2,1,0:T(8,128)S(1)} %get-tuple-element.9.refs_2_, f32[8,16,32,128]{3,2,1,0:T(8,128)S(1)} %get-tuple-element.10.refs_3_, ...), custom_call_target="tpu_custom_call" | custom-call | tf_op jit(solution)/shard_map/combine/pallas_call | solution.py:874

commit v7 on v5

--- a/solution.py
+++ b/solution.py
@@ -67,7 +67,7 @@
     return out
 
 
-def main_kernel(sizes, dims, rhs, sten, x1, r1, p1, s1, t_out, p0, q0, w, ws, s0, diag, q2, scr, csend, crecv,
+def main_kernel(sizes, dims, rhs, sten, x1, r1, p1, s1, t_out, m_out, p0, q0, w, ws, s0, diag, q2, scr, csend, crecv,
                 xsend, xrecv, ysend, yrecv, zsend, zrecv, wzsend, wzrecv, ucross, uw, red, held, gacc, cur, slots,
                 t_alpha, t_beta, t_ib, lsem, xs, xr, ars, arr, ready):
     nf, nx, ny = dims
@@ -763,10 +763,22 @@
         total = sum_end(1)
     with NS("c_alg2"):
         curve = left + mm(alpha_tc, mm(extract(total, 0), alpha))
-        fill(t_out, columns(solve(columns(curve), new, row)))
-
-
-def final_kernel(dims, step, t, x1, r1, p1, s1, sol, res, sol_buf, res_buf, sem):
+        cols = columns(solve(columns(curve), new, row))
+        fill(t_out, cols)
+        slot = lax.rem(lane // 8, 8)
+        high, low = [], []
+        for j in range(8):
+            block = jnp.zeros((8, 128), F32)
+            for i in range(8):
+                block = jnp.where(slot == i, line(cols[j], i), block)
+            block = jnp.where(lax.rem(lane, 8) == row, block, 0.0)
+            near = block.astype(jnp.bfloat16).astype(F32)
+            high.append(near)
+            low.append(jnp.where(lane < 64, block - near, 0.0))
+        m_out[...] = jnp.concatenate(high + low, axis=0).astype(jnp.bfloat16)
+
+
+def final_kernel(dims, step, t, m, x1, r1, p1, s1, sol, res, sol_buf, res_buf, sem):
     nf, nx, ny = dims
 
     def saves(n):
@@ -774,17 +786,25 @@
         return [pltpu.make_async_copy(sol_buf.at[:, part], sol.at[:, part], sem.at[0]),
                 pltpu.make_async_copy(res_buf.at[:, part], res.at[:, part], sem.at[1])]
 
+    def halves(v):
+        v = v.reshape(64, 128)
+        high = v.astype(jnp.bfloat16)
+        low = (v - high.astype(F32)).astype(jnp.bfloat16)
+        return jnp.concatenate([high, low], axis=0)
+
+    blocks = [slice(yb * 8, yb * 8 + 8) for yb in range(ny // 8)]
+
     def body(n, carry):
         for k in range(step):
             x = n * step + k
-            for yb in range(ny // 8):
-                y = slice(yb * 8, yb * 8 + 8)
-                u, v = p1[:, x, y], s1[:, x, y]
-                s, e = x1[:, x, y], r1[:, x, y]
+            both = jnp.concatenate([halves(p1[:, x, y]) for y in blocks], axis=1)
+            moves = jnp.dot(m[...], both, preferred_element_type=F32)
+            moves = moves[:64] + moves[64:]
+            for b, y in enumerate(blocks):
+                v, e = s1[:, x, y], r1[:, x, y]
                 for i in range(nf):
-                    s = s + t[i] * u[i][None]
                     e = e - t[i] * v[i][None]
-                sol_buf[:, x, y] = s
+                sol_buf[:, x, y] = x1[:, x, y] + moves[:, b * 128 : b * 128 + 128].reshape(8, 8, 128)
                 res_buf[:, x, y] = e
         for copy in saves(n):
             copy.start()
@@ -811,11 +831,11 @@
     def kernel(*refs):
         main_kernel(sizes, (nf, nx, ny), *refs)
 
-    x1, r1, p1, s1, t = pl.pallas_call(
+    x1, r1, p1, s1, t, m = pl.pallas_call(
         kernel,
-        out_shape=(kept, kept, kept, kept, table),
+        out_shape=(kept, kept, kept, kept, table, pltpu.VMEM((128, 128), jnp.bfloat16)),
         in_specs=[pl.BlockSpec(memory_space=pltpu.HBM)] * 2,
-        out_specs=(local,) * 5,
+        out_specs=(local,) * 6,
         scratch_shapes=[
             padded, padded,
             pltpu.VMEM((13, nx + 1, tall, nz), F32),
@@ -854,7 +874,7 @@
         name="krylov",
     )(*[pltpu.with_memory_space_constraint(v, pltpu.HBM) for v in (rhs, stencil)])
 
-    step = 2
+    step = 4
 
     def last(*refs):
         final_kernel((nf, nx, ny), step, *refs)
@@ -862,7 +882,7 @@
     return pl.pallas_call(
         last,
         out_shape=(field, field),
-        in_specs=[local] * 5,
+        in_specs=[local] * 6,
         out_specs=(pl.BlockSpec(memory_space=pltpu.HBM),) * 2,
         scratch_shapes=[
             pltpu.VMEM(rhs.shape, F32), pltpu.VMEM(rhs.shape, F32),
@@ -870,7 +890,7 @@
         ],
         compiler_params=pltpu.CompilerParams(vmem_limit_bytes=40 * 2**20),
         name="combine",
-    )(t, x1, r1, p1, s1)
+    )(t, m, x1, r1, p1, s1)
 
 
 def solution(mesh):

time: 39.2 us -> 39 us (level)
  no operation moved by 1% of the time
where the time goes in v7:
time: 39 us; the launch traced here: 38.8 us
  Pallas kernels  38.2 us (98%)
  between operations  0.64 us (2%)
    pallas_call x1, Pallas kernels, shards(): pl.pallas_call(kernel, out_shape=(kept, kept, kept, kept, table, pltpu.VM...  35.3 us
    pallas_call x1, Pallas kernels, shards(): pl.pallas_call(last, out_shape=(field, field), in_specs=[local] * 6, out_...  2.88 us

profile of v7, /device:TPU:0, one launch (start us, length us, event | category | flops | bytes accessed | tf_op | source)
XLA Modules:
  0.0 38.8 jit_solution(4511330735825617845)
XLA Ops:
  0.6 35.3 %krylov.1 = (f32[8,16,32,128]{3,2,1,0:T(8,128)S(1)}, f32[8,16,32,128]{3,2,1,0:T(8,128)S(1)}, f32[8,16,32,128]{3,2,1,0:T(8,128)S(1)}, f32[8,16,32,128]{3,2,1,0:T(...) custom-call(f32[8,16,32,128]{3,2,1,0:T(8,128)} %refs_0_.1, f32[14,16,32,128]{3,2,1,0:T(8,128)} %refs_1_.1), custom_call_target="tpu_custom_call" | custom-call | tf_op jit(solution)/shard_map/krylov/pallas_call | solution.py:834
  35.9 2.9 %combine.1 = (f32[8,16,32,128]{3,2,1,0:T(8,128)}, f32[8,16,32,128]{3,2,1,0:T(8,128)}) custom-call(f32[8,8,8,128]{3,2,1,0:T(8,128)S(1)} %get-tuple-element.8.refs_0_, bf16[128,128]{1,0:T(8,128)(2,1)S(1)} %get-tuple-element.9.refs_1_, f32[8,16,32,128]{3,2,1,0:T(8,128)S(1)} %get-tuple-element.10.refs_2_, f32[8,16,32,128]{3,2,1,0:T(8,128)S(1)} %get-tuple-element.11.refs_3_, ...), custom_call_target="tpu_custom_call" | custom-call | tf_op jit(solution)/shard_map/combine/pallas_call | solution.py:882
